TPU v7x, 512 devices: a 4x2x32 block of a 4x8x32 slice. The times are simulated.
512 devices in a mesh: grp: 2 (over y), gy: 32 (over z), gx: 4 (over x), gz: 2 (over core).
Axes of the slice: x: 4, y: 2, z: 32, core: 2. Of those that a mesh axis runs over, the one named last changes fastest.
The devices are a block of a 4x8x32 slice.
Arguments:
- pair: bfloat16 [1024, 512, 128], P(('grp', 'gx', 'gz'), 'gy'), parts along dimension 0, may hold values from -6 to 6
- lengths: int32 [2], P('grp'), parts along dimension 0, may hold values from 256 to 512
- ln_gain: float32 [128], replicated, may hold values from 0.1 to 1.9
- ln_bias: float32 [128], replicated, may hold values from -3 to 3
- w_ab: bfloat16 [128, 512], replicated, may hold values from -0.5 to 0.5
- w_gate: bfloat16 [128, 128], replicated, may hold values from -0.5 to 0.5
- out_gain: float32 [128], replicated, may hold values from 0.1 to 1.9
- out_bias: float32 [128], replicated, may hold values from -3 to 3
- w_out: bfloat16 [128, 128], replicated, may hold values from -0.5 to 0.5
Outputs:
- update: bfloat16 [1024, 512, 128], P(('grp', 'gx', 'gz'), 'gy'), parts along dimension 0
There are 2 independent parts, one for each index of `grp`. A program takes and returns all parts, laid end to end along the dimension named above; an argument that names none is the same for every part. Nothing has to cross between parts.
Inputs may be any that keep to these rules, and one draw needn't show every extreme that they name: Residues from lengths[0] on are padding.
All inputs are finite; a program needn't handle non-finite values.
Results may differ from a plain program's by a relative error of at most 0.0052.
Values may be sent and summed in bfloat16 or wider, within the bound.
No kernel may reach another device: no remote copies, remote signals or barrier semaphores. Data moves between devices by JAX's collectives and lax.ppermute only.
A program may use at most 128 MiB of HBM per device.

v0:
```python
import jax
import jax.numpy as jnp
from jax import lax
from jax.sharding import PartitionSpec as P


def from_everyone(value, axis):
    copies = jnp.broadcast_to(value, (lax.axis_size(axis), *value.shape))
    return lax.all_to_all(copies, axis, split_axis=0, concat_axis=0, tiled=True)


def in_order(tiles, dim):
    shape = list(tiles.shape[1:])
    shape[dim] *= tiles.shape[0]
    return jnp.moveaxis(tiles, 0, dim).reshape(shape)


def collect(value, axis, dim):
    tiles = from_everyone(value, axis)
    return in_order(tiles, dim)


def layer_norm(values, gain, bias):
    values = values.astype(jnp.float32)
    mean = jnp.mean(values, -1, keepdims=True)
    spread = jnp.mean(jnp.square(values - mean), -1, keepdims=True)
    return (values - mean) * lax.rsqrt(spread + 1e-05) * gain + bias


def channel_norm(values, gain, bias):
    mean = jnp.mean(values, 0, keepdims=True)
    spread = jnp.mean(jnp.square(values - mean), 0, keepdims=True)
    return (values - mean) * lax.rsqrt(spread + 1e-05) * gain[:, None, None] + bias[:, None, None]


def body(pair, lengths, ln_gain, ln_bias, w_ab, w_gate, out_gain, out_bias, w_out):
    tile_rows, tile_cols, width = pair.shape
    hidden = w_out.shape[0]
    row_start = lax.axis_index(("gx", "gz")) * tile_rows
    col_index = lax.axis_index("gy")
    col_start = col_index * tile_cols
    normed = layer_norm(pair, ln_gain, ln_bias).astype(jnp.bfloat16)
    flat = normed.reshape(tile_rows * tile_cols, width)
    proj = jnp.dot(flat, w_ab, preferred_element_type=jnp.float32).reshape(
        tile_rows, tile_cols, 4 * hidden
    )
    row_live = (row_start + jnp.arange(tile_rows, dtype=jnp.int32) < lengths[0]).astype(jnp.float32)
    col_live = (col_start + jnp.arange(tile_cols, dtype=jnp.int32) < lengths[0]).astype(jnp.float32)
    pair_mask = (row_live[:, None] * col_live[None, :])[..., None]
    left = (pair_mask * jax.nn.sigmoid(proj[..., :hidden]) * proj[..., hidden : 2 * hidden]).astype(
        jnp.bfloat16
    )
    right = (
        pair_mask * jax.nn.sigmoid(proj[..., 2 * hidden : 3 * hidden]) * proj[..., 3 * hidden :]
    ).astype(jnp.bfloat16)
    left_major = jnp.transpose(left, (2, 0, 1))
    right_major = jnp.transpose(right, (2, 0, 1))
    column_rows = collect(right_major, ("gx", "gz"), 1)
    right_mine = lax.all_to_all(column_rows, "gy", split_axis=1, concat_axis=2, tiled=True)
    triangle = jnp.einsum(
        "cik,cjk->cij",
        lax.all_gather(left_major, "gy", axis=2, tiled=True),
        right_mine,
        preferred_element_type=jnp.float32,
    )
    tri_norm = channel_norm(triangle, out_gain, out_bias).astype(jnp.bfloat16)
    gate = jax.nn.sigmoid(jnp.dot(flat, w_gate, preferred_element_type=jnp.float32)).reshape(
        tile_rows, tile_cols, width
    )
    projected = jnp.einsum("cij,cd->ijd", tri_norm, w_out, preferred_element_type=jnp.float32)
    return (gate * projected).astype(jnp.bfloat16)


def solution(mesh):
    in_specs = (P(("grp", "gx", "gz"), "gy", None), P("grp"), P(), P(), P(), P(), P(), P(), P())
    out_specs = P(("grp", "gx", "gz"), "gy", None)
    return jax.shard_map(body, mesh=mesh, in_specs=in_specs, out_specs=out_specs, check_vma=False)
```

profile of v0, /device:TPU:38, one launch (start us, length us, event | category | flops | bytes accessed | tf_op | source)
XLA Modules:
  0.0 450.6 jit_solution(10846532416130291619)
XLA Ops:
  6.5 0.0 copy-start
  7.2 1.2 convert_reduce_fusion
  8.4 0.1 copy.35
  8.5 0.1 copy.36
  8.6 1.3 fusion.6
  9.9 0.1 copy.37
  10.0 0.1 copy.38
  10.1 0.1 broadcast_multiply_fusion
  10.2 1.3 fusion.9
  11.5 0.0 copy-done
  11.5 0.4 fusion.22
  11.9 1.0 fusion.21
  12.9 1.6 broadcast_in_dim.2
  14.5 44.4 %all-to-all-start = ((bf16[8,128,64,16]{1,3,2,0:T(8,128)(2,1)}), bf16[8,128,64,16]{1,3,2,0:T(8,128)(2,1)}, u32[]{:S(2)}, u32[]{:S(2)}) async-start(bf16[8,128,64,16]{1,3,2,0:T(8,128)(2,1)} %broadcast_in_dim.2), calls=%async_computation | async-start | bytes 4194304 | tf_op jit(solution)/shard_map/all_to_all | solution.py:9
  59.0 0.0 all-gather.2.cloned.1.call-start
  59.0 0.7 all-gather.2.cloned.1.call-update
  59.7 24.4 %all-to-all-done = bf16[8,128,64,16]{1,3,2,0:T(8,128)(2,1)} async-done(((bf16[8,128,64,16]{1,3,2,0:T(8,128)(2,1)}), bf16[8,128,64,16]{1,3,2,0:T(8,128)(2,1)}, u32[]{:S(2)}, u32[]{:S(2)}) %all-to-all-start) | async-done | bytes 2097184 | tf_op jit(solution)/shard_map/all_to_all | solution.py:9
  84.1 0.0 copy-start.4
  84.1 6.2 %all-to-all-start.1 = ((bf16[128,512,16]{0,2,1:T(8,128)(2,1)}), bf16[128,512,16]{0,2,1:T(8,128)(2,1)S(1)}, u32[]{:S(2)}, u32[]{:S(2)}) async-start(bf16[128,512,16]{0,2,1:T(8,128)(2,1)} %bitcast.7), calls=%async_computation.1 | async-start | bytes 4194304 | tf_op jit(solution)/shard_map/all_to_all | solution.py:59
  90.3 0.0 copy-done.4
  90.3 0.3 fusion.2
  90.6 309.4 %all-gather.2.cloned.1.call-done = bf16[128,64,512]{0,2,1:T(8,128)(2,1)} async-done(((bf16[128,64,16]{0,2,1:T(8,128)(2,1)}), bf16[128,64,512]{0,2,1:T(8,128)(2,1)}) %all-gather.2.cloned.1.call-update) | async-done | bytes 8388624 | tf_op jit(solution)/shard_map/all_gather | solution.py:62
  400.0 29.2 %copy.40 = bf16[128,64,512]{1,2,0:T(8,128)(2,1)} copy(bf16[128,64,512]{0,2,1:T(8,128)(2,1)} %all-gather.2.cloned.1.call-done) | data formatting | bytes 16777216 | tf_op jit(solution)/shard_map/all_gather | solution.py:62
  429.2 0.0 all-to-all-done.1
  429.2 1.9 copy.39
  431.1 3.4 copy.41
  434.5 0.0 copy-start.2
  434.5 0.0 copy-start.3
  434.5 7.1 %fusion.25 = (f32[64,16]{0,1:T(8,128)S(1)}, f32[128,64,16]{1,2,0:T(8,128)S(1)}) fusion(bf16[128,16,512]{2,1,0:T(8,128)(2,1)S(1)} %copy.41, bf16[128,64,512]{1,2,0:T(8,128)(2,1)} %copy.40), kind=kOutput, calls=%fused_computation.42 | convolution fusion | flops 134347776 | bytes 11014144 | tf_op jit(solution)/shard_map/cik,cjk->cij/dot_general | solution.py:60
  441.6 0.0 copy-start.1
  441.6 0.2 multiply_reduce_fusion
  441.8 0.0 copy-done.2
  441.8 0.0 copy-done.3
  441.8 0.3 add_convert_fusion
  442.2 0.6 copy.42
  442.8 0.0 copy-done.1
  442.8 0.9 fusion.3
  (6 shorter events, 0.0 us)
Async XLA Ops:
  6.5 4.9 %copy-start = (bf16[128,512]{1,0:T(8,128)(2,1)S(1)}, bf16[128,512]{1,0:T(8,128)(2,1)}, u32[]{:S(2)}) copy-start(bf16[128,512]{1,0:T(8,128)(2,1)} %param.13) | copy-start | bytes 393220
  14.5 69.6 %all-to-all-start = ((bf16[8,128,64,16]{1,3,2,0:T(8,128)(2,1)}), bf16[8,128,64,16]{1,3,2,0:T(8,128)(2,1)}, u32[]{:S(2)}, u32[]{:S(2)}) async-start(bf16[8,128,64,16]{1,3,2,0:T(8,128)(2,1)} %broadcast_in_dim.2), calls=%async_computation | async-start | bytes 4194304 | tf_op jit(solution)/shard_map/all_to_all | solution.py:9
  59.0 341.1 %all-gather.2.cloned.1.call-start = ((), (), s32[]{:S(2)}) async-start(), calls=%async_computation.2 | async-start | bytes 8650752 | tf_op jit(solution)/shard_map/all_gather | solution.py:62
  84.1 6.2 %copy-start.4 = (bf16[128,128]{1,0:T(8,128)(2,1)S(1)}, bf16[128,128]{1,0:T(8,128)(2,1)}, u32[]{:S(2)}) copy-start(bf16[128,128]{1,0:T(8,128)(2,1)} %param.14) | copy-start | bytes 98308
  84.1 345.1 %all-to-all-start.1 = ((bf16[128,512,16]{0,2,1:T(8,128)(2,1)}), bf16[128,512,16]{0,2,1:T(8,128)(2,1)S(1)}, u32[]{:S(2)}, u32[]{:S(2)}) async-start(bf16[128,512,16]{0,2,1:T(8,128)(2,1)} %bitcast.7), calls=%async_computation.1 | async-start | bytes 4194304 | tf_op jit(solution)/shard_map/all_to_all | solution.py:59
  434.5 7.3 %copy-start.2 = (f32[128]{0:T(128)S(1)}, f32[128]{0:T(128)}, u32[]{:S(2)}) copy-start(f32[128]{0:T(128)} %param.16) | copy-start | bytes 1540
  434.5 7.3 %copy-start.3 = (f32[128]{0:T(128)S(1)}, f32[128]{0:T(128)}, u32[]{:S(2)}) copy-start(f32[128]{0:T(128)} %param.15) | copy-start | bytes 1540
  441.6 1.2 copy-start.1
Sparse Core Ops, SparseCore 0:
  61.8 338.2 all-gather.1
where the time goes:
time: 455 us; the launch traced here: 451 us
  waiting for transfers between devices  335 us (74%)
  starting transfers between devices  50.6 us (11%)
  local copies, waits for them, and re-layouts  37 us (8%)
  between operations  14.3 us (3%)
  matrix products  8.67 us (2%)
  other arithmetic  5.46 us (1%)
    all_gather x1, waiting for transfers between devices, body(): lax.all_gather(left_major, 'gy', axis=2, tiled=True)  309 us
    all_to_all x1, starting transfers between devices, from_everyone(): return lax.all_to_all(copies, axis, split_axis=0, concat_axis=0, tiled=True)  44.4 us
    all_gather x1, local copies, waits for them, and re-layouts, body(): lax.all_gather(left_major, 'gy', axis=2, tiled=True)  29.2 us
    all_to_all x1, waiting for transfers between devices, from_everyone(): return lax.all_to_all(copies, axis, split_axis=0, concat_axis=0, tiled=True)  24.4 us
  transfers between devices with their start and end apart: 3, of which 2 were waited for; matrix products, arithmetic and copies ran while one was open for 7% of the time, Pallas kernels for 0%

commit v1 on v0

v1 whole, which is shorter than its diff:
```python
import functools

import jax
import jax.numpy as jnp
from jax import lax
from jax.experimental import pallas as pl
from jax.experimental.pallas import tpu as pltpu
from jax.sharding import PartitionSpec as P

NT = (((1,), (1,)), ((), ()))
TN = (((0,), (0,)), ((), ()))
EPS = 1e-05


def low_half(shape):
    return lax.broadcasted_iota(jnp.int32, shape, len(shape) - 1) < shape[-1] // 2


def swap_halves(value):
    return pltpu.roll(value, value.shape[-1] // 2, value.ndim - 1)


def pre_kernel(place, length, x_ref, gain, bias, w_ref, normed_ref, out_ref, rows_s, out_s):
    rows, cols, width = x_ref.shape
    hidden = w_ref.shape[1] // 4
    x = x_ref[...].reshape(rows * cols, width).astype(jnp.float32)
    mean = jnp.mean(x, -1, keepdims=True)
    x = x - mean
    spread = jnp.mean(x * x, -1, keepdims=True)
    normed = (x * lax.rsqrt(spread + EPS) * gain[...] + bias[...]).astype(jnp.bfloat16)
    normed_ref[...] = normed
    rows_s[...] = normed.astype(jnp.float32)
    w_t = w_ref[...].astype(jnp.float32).T.astype(jnp.bfloat16)
    low = low_half((1, 2 * rows))
    lane = lax.broadcasted_iota(jnp.int32, (1, 2 * rows), 1)
    row_live = place[0] + jnp.where(low, lane, lane - rows) < length[0]
    for pair in range(cols // 2):
        k = 2 * pair
        block = jnp.concatenate(
            [rows_s[pl.ds(k, rows, stride=cols), :], rows_s[pl.ds(k + 1, rows, stride=cols), :]], 0
        ).astype(jnp.bfloat16)
        proj = lax.dot_general(w_t, block, NT, preferred_element_type=jnp.float32)
        col_live = place[1] + k + jnp.where(low, 0, 1) < length[0]
        mask = jnp.where(row_live & col_live, 1.0, 0.0)
        left = mask * jax.nn.sigmoid(proj[:hidden]) * proj[hidden : 2 * hidden]
        right = mask * jax.nn.sigmoid(proj[2 * hidden : 3 * hidden]) * proj[3 * hidden :]
        out_s[pl.ds(k, hidden, stride=cols), :] = jnp.where(low, left, swap_halves(right))
        out_s[pl.ds(k + 1, hidden, stride=cols), :] = jnp.where(low, swap_halves(left), right)
    out_ref[...] = out_s[...].astype(jnp.bfloat16).reshape(out_ref.shape)


def mid_kernel(place, own_ref, peer_ref, out_ref):
    steps, blocks, depth, lanes = own_ref.shape
    half = lanes // 2

    def operand(ref, first):
        parts = [ref[:, x].reshape(steps * depth, lanes)[:, first : first + half] for x in range(blocks)]
        return jnp.concatenate(parts, 1)

    left = operand(own_ref, 0)
    low = low_half((1, 1, lanes))
    for which, ref in enumerate((own_ref, peer_ref)):
        core = place[2] if which == 0 else 1 - place[2]
        total = lax.dot_general(operand(ref, half), left, TN, preferred_element_type=jnp.float32)
        total = total.reshape(blocks * half // depth, depth, blocks * half)
        top, bottom = total[:, : depth // 2], total[:, depth // 2 :]
        for pair in range(blocks // 2):
            here = slice(pair * lanes, (pair + 1) * lanes)
            even = jnp.where(low, top[..., here], swap_halves(bottom[..., here]))
            odd = jnp.where(low, swap_halves(top[..., here]), bottom[..., here])
            tiles = jnp.concatenate([even, odd], 1).astype(jnp.bfloat16)
            out_ref[:, core, :, pair] = tiles.reshape(blocks, half // depth, depth, lanes)


def post_kernel(t_ref, gate, gain, bias, w_ref, out_ref, t_s, out_s):
    rows, cols, width = out_ref.shape
    hidden = w_ref.shape[0]
    depth = cols // 2
    t_s[...] = t_ref[...].astype(jnp.float32).reshape(t_s.shape)
    gain_t = jnp.broadcast_to(gain[...], (2 * rows, hidden)).T
    bias_t = jnp.broadcast_to(bias[...], (2 * rows, hidden)).T
    w = w_ref[...]
    for r in range(depth):
        t = t_s[pl.ds(r, hidden, stride=depth), :]
        t = t - jnp.mean(t, 0, keepdims=True)
        spread = jnp.mean(t * t, 0, keepdims=True)
        t = (t * lax.rsqrt(spread + EPS) * gain_t + bias_t).astype(jnp.bfloat16)
        o = lax.dot_general(t, w, TN, preferred_element_type=jnp.float32)
        out_s[pl.ds(r, rows, stride=cols), :] = o[:rows]
        out_s[pl.ds(depth + r, rows, stride=cols), :] = o[rows:]
    out_ref[...] = (gate[...] * out_s[...]).astype(jnp.bfloat16).reshape(out_ref.shape)


SMEM = pl.BlockSpec(memory_space=pltpu.SMEM)
VMEM = pl.BlockSpec(memory_space=pltpu.VMEM)


def body(pair, lengths, ln_gain, ln_bias, w_ab, w_gate, out_gain, out_bias, w_out):
    rows, cols, width = pair.shape
    hidden = w_out.shape[0]
    steps, blocks, cores = (lax.axis_size(a) for a in ("gy", "gx", "gz"))
    place = jnp.stack(
        [lax.axis_index(("gx", "gz")) * rows, lax.axis_index("gy") * cols, lax.axis_index("gz")]
    ).astype(jnp.int32)
    normed, operands = pl.pallas_call(
        pre_kernel,
        out_shape=(
            jax.ShapeDtypeStruct((rows * cols, width), jnp.bfloat16),
            jax.ShapeDtypeStruct((hidden, cols, 2 * rows), jnp.bfloat16),
        ),
        in_specs=[SMEM, SMEM, VMEM, VMEM, VMEM, VMEM],
        out_specs=(VMEM, VMEM),
        scratch_shapes=[
            pltpu.VMEM((rows * cols, width), jnp.float32),
            pltpu.VMEM((hidden * cols, 2 * rows), jnp.float32),
        ],
        name="pre",
    )(place, lengths, pair, ln_gain[None], ln_bias[None], w_ab)
    own = lax.all_to_all(operands, ("gy", "gx"), 0, 0, tiled=True)
    peer = lax.ppermute(own, "gz", [(g, cores - 1 - g) for g in range(cores)])
    gate = jax.nn.sigmoid(jnp.dot(normed, w_gate, preferred_element_type=jnp.float32))
    shape = (steps, blocks, cols, 2 * rows)
    tiles = pl.pallas_call(
        mid_kernel,
        out_shape=jax.ShapeDtypeStruct(
            (blocks, cores, rows // cols, blocks // 2, cols, 2 * rows), jnp.bfloat16
        ),
        in_specs=[SMEM, VMEM, VMEM],
        out_specs=VMEM,
        name="mid",
    )(place, own.reshape(shape), peer.reshape(shape))
    tiles = tiles.reshape(steps * blocks, cols // 2, 2 * rows)
    back = lax.all_to_all(tiles, ("gy", "gx"), 0, 0, tiled=True)
    return pl.pallas_call(
        post_kernel,
        out_shape=jax.ShapeDtypeStruct((rows, cols, width), jnp.bfloat16),
        in_specs=[VMEM] * 5,
        out_specs=VMEM,
        scratch_shapes=[
            pltpu.VMEM((hidden * cols // 2, 2 * rows), jnp.float32),
            pltpu.VMEM((rows * cols, width), jnp.float32),
        ],
        name="post",
    )(back.reshape(hidden // 2, cols, 2 * rows), gate, out_gain[None], out_bias[None], w_out)


def solution(mesh):
    in_specs = (P(("grp", "gx", "gz"), "gy", None), P("grp"), P(), P(), P(), P(), P(), P(), P())
    out_specs = P(("grp", "gx", "gz"), "gy", None)
    return jax.shard_map(body, mesh=mesh, in_specs=in_specs, out_specs=out_specs, check_vma=False)
```

time: 455 us -> 179 us (0.39)
  waiting for transfers between devices: 335 us -> 41.4 us
  blocking collectives: 0 us -> 113 us
  starting transfers between devices: 50.6 us -> 12 us
  local copies, waits for them, and re-layouts: 37 us -> 1.52 us
  between operations: 14.3 us -> 0.7 us
  Pallas kernels: 0 us -> 8.18 us
  matrix products: 8.67 us -> 1.1 us
  other arithmetic: 5.46 us -> 0.65 us
    all_gather x1 -> x0, waiting for transfers between devices: 309 us -> none  [body(): lax.all_gather(left_major, 'gy', axis=2, tiled=True)]
    all_to_all x0 -> x1, blocking collectives: none -> 113 us  [body(): own = lax.all_to_all(operands, ('gy', 'gx'), 0, 0, tiled=True)]
    all_to_all x2 -> x1, starting transfers between devices: 50.6 us -> 10 us  [body(): back = lax.all_to_all(tiles, ('gy', 'gx'), 0, 0, tiled=True)]
    all_gather x1 -> x0, local copies, waits for them, and re-layouts: 29.2 us -> none  [body(): lax.all_gather(left_major, 'gy', axis=2, tiled=True)]
    all_to_all x2 -> x1, waiting for transfers between devices: 24.4 us -> 39.5 us  [body(): back = lax.all_to_all(tiles, ('gy', 'gx'), 0, 0, tiled=True)]
    pallas_call x0 -> x3, Pallas kernels: none -> 8.18 us  [the longest x1 3.11 us: body(): pl.pallas_call(pre_kernel, out_shape=(jax.ShapeDtypeStruct((rows * cols,...]
    dot_general x4 -> x1, matrix products: 8.67 us -> 1.1 us  [body(): jnp.dot(normed, w_gate, preferred_element_type=jnp.float32)]
    all_to_all x2 -> x0, local copies, waits for them, and re-layouts: 5.31 us -> none  [body(): lax.all_to_all(column_rows, 'gy', split_axis=1, concat_axis=2, tiled=True)]
  transfers between devices with their start and end apart: 3 -> 2, of which waited for: 2 -> 2; matrix products, arithmetic and copies ran while one was open for 7% -> 1% of each run, Pallas kernels for 0% -> 0%
where the time goes in v1:
time: 179 us; the launch traced here: 178 us
  blocking collectives  113 us (63%)
  waiting for transfers between devices  41.4 us (23%)
  starting transfers between devices  12 us (7%)
  Pallas kernels  8.18 us (5%)
    all_to_all x1, blocking collectives, body(): own = lax.all_to_all(operands, ('gy', 'gx'), 0, 0, tiled=True)  113 us
    all_to_all x1, waiting for transfers between devices, body(): back = lax.all_to_all(tiles, ('gy', 'gx'), 0, 0, tiled=True)  39.5 us
    all_to_all x1, starting transfers between devices, body(): back = lax.all_to_all(tiles, ('gy', 'gx'), 0, 0, tiled=True)  10 us
  transfers between devices with their start and end apart: 2, of which 2 were waited for; matrix products, arithmetic and copies ran while one was open for 1% of the time, Pallas kernels for 0%

profile of v1, /device:TPU:38, one launch (start us, length us, event | category | flops | bytes accessed | tf_op | source)
XLA Modules:
  0.0 178.2 jit_solution(16071152606230435569)
XLA Ops:
  0.0 0.0 copy-start
  0.7 0.7 pad_add_fusion.place
  1.3 3.1 %pre.1 = (bf16[1024,128]{1,0:T(8,128)(2,1)}, bf16[128,16,128]{2,1,0:T(8,128)(2,1)}) custom-call(s32[3]{0:T(128)} %pad_add_fusion.place, s32[1]{0:T(128)S(6)} %copy.10.length, bf16[64,16,128]{2,1,0:T(8,128)(2,1)} %x_ref.1, f32[1,128]{1,0:T(1,128)} %bitcast.19, f32[1,128]{1,0:T(1,128)} %bitcast.20, bf16[128,512]{1,0:T(8,128)(2,1)} %w_ref.2), custom_call_target="tpu_custom_call" | custom-call | tf_op jit(solution)/shard_map/pre/pallas_call | solution.py:105
  4.4 112.7 %all_to_all.10 = bf16[128,16,128]{2,1,0:T(8,128)(2,1)S(1)} all-to-all(bf16[128,16,128]{2,1,0:T(8,128)(2,1)} %get-tuple-element.7), channel_id=1, replica_groups=mesh['grp'=2,'gy'=32,'gx'=4,'gz'=2] {'gy','gx'}, dimensions={0} | all-to-all | bytes 1048576 | tf_op jit(solution)/shard_map/all_to_all | solution.py:119
  117.2 0.0 copy-start.1
  117.2 1.9 %collective-permute-start = (bf16[128,16,128]{2,1,0:T(8,128)(2,1)S(1)}, bf16[128,16,128]{2,1,0:T(8,128)(2,1)S(1)}, u32[]{:S(2)}, u32[]{:S(2)}) collective-permute-start(bf16[128,16,128]{2,1,0:T(8,128)(2,1)S(1)} %all_to_all.10), channel_id=1, source_target_pairs={{0,1},{1,0},{2,3},{3,2},{4,5},{5,4},{6,7},{7,6},{8,9},{9,8},{10,11... | collective-permute-start | bytes 1572872 | tf_op jit(solution)/shard_map/ppermute | solution.py:120
  119.1 1.9 %collective-permute-done = bf16[128,16,128]{2,1,0:T(8,128)(2,1)S(1)} collective-permute-done((bf16[128,16,128]{2,1,0:T(8,128)(2,1)S(1)}, bf16[128,16,128]{2,1,0:T(8,128)(2,1)S(1)}, u32[]{:S(2)}, u32[]{:S(2)}) %collective-permute-start) | collective-permute-done | bytes 524320 | tf_op jit(solution)/shard_map/ppermute | solution.py:120
  121.0 0.0 copy-start.3
  121.0 0.0 copy-done.1
  121.0 0.8 copy-done.3
  121.8 2.7 %mid.1 = bf16[4,2,4,2,16,128]{5,4,3,2,1,0:T(8,128)(2,1)} custom-call(s32[3]{0:T(128)} %pad_add_fusion.place, bf16[32,4,16,128]{3,2,1,0:T(8,128)(2,1)} %bitcast.13, bf16[32,4,16,128]{3,2,1,0:T(8,128)(2,1)} %bitcast.16), custom_call_target="tpu_custom_call" | custom-call | tf_op jit(solution)/shard_map/mid/pallas_call | solution.py:123
  124.5 0.0 copy-start.4
  124.5 10.0 %all-to-all-start.1 = ((bf16[128,8,128]{2,1,0:T(8,128)(2,1)}), bf16[128,8,128]{2,1,0:T(8,128)(2,1)S(1)}, u32[]{:S(2)}, u32[]{:S(2)}) async-start(bf16[128,8,128]{2,1,0:T(8,128)(2,1)} %bitcast.15), calls=%async_computation.1 | async-start | bytes 524288 | tf_op jit(solution)/shard_map/all_to_all | solution.py:133
  134.5 0.0 copy-done
  134.5 0.0 copy-done.4
  134.5 1.1 fusion.2.gate
  135.6 39.5 %all-to-all-done.1 = bf16[128,8,128]{2,1,0:T(8,128)(2,1)S(1)} async-done(((bf16[128,8,128]{2,1,0:T(8,128)(2,1)}), bf16[128,8,128]{2,1,0:T(8,128)(2,1)S(1)}, u32[]{:S(2)}, u32[]{:S(2)}) %all-to-all-start.1) | async-done | bytes 262176 | tf_op jit(solution)/shard_map/all_to_all | solution.py:133
  175.1 0.0 copy-start.2
  175.1 0.7 copy-done.2
  175.8 2.4 %post.1 = bf16[64,16,128]{2,1,0:T(8,128)(2,1)} custom-call(bf16[64,16,128]{2,1,0:T(8,128)(2,1)} %bitcast.14, f32[1024,128]{1,0:T(8,128)} %fusion.2.gate, f32[1,128]{1,0:T(1,128)} %bitcast.17, f32[1,128]{1,0:T(1,128)} %bitcast.18, bf16[128,128]{1,0:T(8,128)(2,1)} %w_ref.3), custom_call_target="tpu_custom_call" | custom-call | tf_op jit(solution)/shard_map/post/pallas_call | solution.py:134
Async XLA Ops:
  0.0 134.5 %copy-start = (bf16[128,128]{1,0:T(8,128)(2,1)S(1)}, bf16[128,128]{1,0:T(8,128)(2,1)}, u32[]{:S(2)}) copy-start(bf16[128,128]{1,0:T(8,128)(2,1)} %param.14) | copy-start | bytes 98308
  117.2 3.8 %copy-start.1 = (bf16[128,16,128]{2,1,0:T(8,128)(2,1)}, bf16[128,16,128]{2,1,0:T(8,128)(2,1)S(1)}, u32[]{:S(2)}) copy-start(bf16[128,16,128]{2,1,0:T(8,128)(2,1)S(1)} %all_to_all.10) | copy-start | bytes 1572868
  117.2 3.8 %collective-permute-start = (bf16[128,16,128]{2,1,0:T(8,128)(2,1)S(1)}, bf16[128,16,128]{2,1,0:T(8,128)(2,1)S(1)}, u32[]{:S(2)}, u32[]{:S(2)}) collective-permute-start(bf16[128,16,128]{2,1,0:T(8,128)(2,1)S(1)} %all_to_all.10), channel_id=1, source_target_pairs={{0,1},{1,0},{2,3},{3,2},{4,5},{5,4},{6,7},{7,6},{8,9},{9,8},{10,11... | collective-permute-start | bytes 1572872 | tf_op jit(solution)/shard_map/ppermute | solution.py:120
  121.0 0.8 copy-start.3
  124.5 10.0 %copy-start.4 = (bf16[1024,128]{1,0:T(8,128)(2,1)S(1)}, bf16[1024,128]{1,0:T(8,128)(2,1)}, u32[]{:S(2)}) copy-start(bf16[1024,128]{1,0:T(8,128)(2,1)} %get-tuple-element.8) | copy-start | bytes 786436
  124.5 50.6 %all-to-all-start.1 = ((bf16[128,8,128]{2,1,0:T(8,128)(2,1)}), bf16[128,8,128]{2,1,0:T(8,128)(2,1)S(1)}, u32[]{:S(2)}, u32[]{:S(2)}) async-start(bf16[128,8,128]{2,1,0:T(8,128)(2,1)} %bitcast.15), calls=%async_computation.1 | async-start | bytes 524288 | tf_op jit(solution)/shard_map/all_to_all | solution.py:133
  175.1 0.7 copy-start.2

commit v2 on v1

v2 whole, which is shorter than its diff:
```python
import functools

import jax
import jax.numpy as jnp
from jax import lax
from jax.experimental import pallas as pl
from jax.experimental.pallas import tpu as pltpu
from jax.sharding import PartitionSpec as P

NT = (((1,), (1,)), ((), ()))
TN = (((0,), (0,)), ((), ()))
EPS = 1e-05


def low_half(shape):
    return lax.broadcasted_iota(jnp.int32, shape, len(shape) - 1) < shape[-1] // 2


def swap_halves(value):
    return pltpu.roll(value, value.shape[-1] // 2, value.ndim - 1)


def pre_kernel(length, x_ref, gain, bias, w_ref, normed_ref, out_ref, rows_s, out_s):
    rows, cols, width = x_ref.shape
    hidden = w_ref.shape[1] // 4
    x = x_ref[...].reshape(rows * cols, width).astype(jnp.float32)
    mean = jnp.mean(x, -1, keepdims=True)
    x = x - mean
    spread = jnp.mean(x * x, -1, keepdims=True)
    normed = (x * lax.rsqrt(spread + EPS) * gain[...] + bias[...]).astype(jnp.bfloat16)
    normed_ref[...] = normed
    rows_s[...] = normed.astype(jnp.float32)
    w_t = w_ref[...].astype(jnp.float32).T.astype(jnp.bfloat16)
    low = low_half((1, 2 * rows))
    lane = lax.broadcasted_iota(jnp.int32, (1, 2 * rows), 1)
    row_start = (lax.axis_index("gx") * lax.axis_size("gz") + lax.axis_index("gz")) * rows
    col_start = lax.axis_index("gy") * cols
    row_live = row_start + jnp.where(low, lane, lane - rows) < length[0]
    for pair in range(cols // 2):
        k = 2 * pair
        block = jnp.concatenate(
            [rows_s[pl.ds(k, rows, stride=cols), :], rows_s[pl.ds(k + 1, rows, stride=cols), :]], 0
        ).astype(jnp.bfloat16)
        proj = lax.dot_general(w_t, block, NT, preferred_element_type=jnp.float32)
        col_live = col_start + k + jnp.where(low, 0, 1) < length[0]
        mask = jnp.where(row_live & col_live, 1.0, 0.0)
        left = mask * jax.nn.sigmoid(proj[:hidden]) * proj[hidden : 2 * hidden]
        right = mask * jax.nn.sigmoid(proj[2 * hidden : 3 * hidden]) * proj[3 * hidden :]
        out_s[pl.ds(k, hidden, stride=cols), :] = jnp.where(low, left, swap_halves(right))
        out_s[pl.ds(k + 1, hidden, stride=cols), :] = jnp.where(low, swap_halves(left), right)
    out_ref[...] = out_s[...].astype(jnp.bfloat16).reshape(out_ref.shape)


def operand(ref, first):
    steps, blocks, depth, lanes = ref.shape
    half = lanes // 2
    parts = [ref[:, x].reshape(steps * depth, lanes)[:, first : first + half] for x in range(blocks)]
    return jnp.concatenate(parts, 1)


def product(left, right, depth):
    lanes = 2 * left.shape[1] // 4
    half = lanes // 2
    low = low_half((1, 1, lanes))
    total = lax.dot_general(right, left, TN, preferred_element_type=jnp.float32)
    blocks = total.shape[1] // half
    total = total.reshape(total.shape[0] // depth, depth, blocks * half)
    top, bottom = total[:, : depth // 2], total[:, depth // 2 :]
    tiles = []
    for pair in range(blocks // 2):
        here = slice(pair * lanes, (pair + 1) * lanes)
        even = jnp.where(low, top[..., here], swap_halves(bottom[..., here]))
        odd = jnp.where(low, swap_halves(top[..., here]), bottom[..., here])
        tiles.append(jnp.concatenate([even, odd], 1).astype(jnp.bfloat16))
    return [t.reshape(blocks, t.shape[0] // blocks, depth, lanes) for t in tiles]


def own_kernel(own_ref, out_ref):
    half = own_ref.shape[3] // 2
    tiles = product(operand(own_ref, 0), operand(own_ref, half), own_ref.shape[2])
    for pair, tile in enumerate(tiles):
        out_ref[:, :, pair] = tile


def peer_kernel(own_ref, peer_ref, done_ref, out_ref):
    half = own_ref.shape[3] // 2
    core = lax.axis_index("gz")
    out_ref[:, core] = done_ref[...]
    tiles = product(operand(own_ref, 0), operand(peer_ref, half), own_ref.shape[2])
    for pair, tile in enumerate(tiles):
        out_ref[:, 1 - core, :, pair] = tile


def post_kernel(t_ref, normed, w_gate, gain, bias, w_ref, out_ref, t_s, out_s):
    rows, cols, width = out_ref.shape
    hidden = w_ref.shape[0]
    depth = cols // 2
    t_s[...] = t_ref[...].astype(jnp.float32).reshape(t_s.shape)
    gain_t = jnp.broadcast_to(gain[...], (2 * rows, hidden)).T
    bias_t = jnp.broadcast_to(bias[...], (2 * rows, hidden)).T
    w = w_ref[...]
    for r in range(depth):
        t = t_s[pl.ds(r, hidden, stride=depth), :]
        t = t - jnp.mean(t, 0, keepdims=True)
        spread = jnp.mean(t * t, 0, keepdims=True)
        t = (t * lax.rsqrt(spread + EPS) * gain_t + bias_t).astype(jnp.bfloat16)
        o = lax.dot_general(t, w, TN, preferred_element_type=jnp.float32)
        out_s[pl.ds(r, rows, stride=cols), :] = o[:rows]
        out_s[pl.ds(depth + r, rows, stride=cols), :] = o[rows:]
    gate = jax.nn.sigmoid(jnp.dot(normed[...], w_gate[...], preferred_element_type=jnp.float32))
    out_ref[...] = (gate * out_s[...]).astype(jnp.bfloat16).reshape(out_ref.shape)


SMEM = pl.BlockSpec(memory_space=pltpu.SMEM)
VMEM = pl.BlockSpec(memory_space=pltpu.VMEM)
PARAMS = pltpu.CompilerParams(vmem_limit_bytes=16 * 2**20)


def body(pair, lengths, ln_gain, ln_bias, w_ab, w_gate, out_gain, out_bias, w_out):
    rows, cols, width = pair.shape
    hidden = w_out.shape[0]
    steps, blocks, cores = (lax.axis_size(a) for a in ("gy", "gx", "gz"))
    normed, operands = pl.pallas_call(
        pre_kernel,
        out_shape=(
            jax.ShapeDtypeStruct((rows * cols, width), jnp.bfloat16),
            jax.ShapeDtypeStruct((hidden, cols, 2 * rows), jnp.bfloat16),
        ),
        in_specs=[SMEM, VMEM, VMEM, VMEM, VMEM],
        compiler_params=PARAMS,
        out_specs=(VMEM, VMEM),
        scratch_shapes=[
            pltpu.VMEM((rows * cols, width), jnp.float32),
            pltpu.VMEM((hidden * cols, 2 * rows), jnp.float32),
        ],
        name="pre",
    )(lengths, pair, ln_gain[None], ln_bias[None], w_ab)
    own = lax.all_to_all(operands, ("gy", "gx"), 0, 0, tiled=True)
    peer = lax.ppermute(own, "gz", [(g, cores - 1 - g) for g in range(cores)])
    shape = (steps, blocks, cols, 2 * rows)
    own, peer = own.reshape(shape), peer.reshape(shape)
    group = (blocks, rows // cols, blocks // 2, cols, 2 * rows)
    tiles = pl.pallas_call(
        own_kernel,
        out_shape=jax.ShapeDtypeStruct(group, jnp.bfloat16),
        in_specs=[VMEM],
        out_specs=VMEM,
        compiler_params=PARAMS,
        cost_estimate=pl.CostEstimate(flops=2**30, bytes_accessed=2**20, transcendentals=0),
        name="own",
    )(own)
    tiles = pl.pallas_call(
        peer_kernel,
        out_shape=jax.ShapeDtypeStruct((blocks, cores, *group[1:]), jnp.bfloat16),
        in_specs=[VMEM] * 3,
        out_specs=VMEM,
        compiler_params=PARAMS,
        name="peer",
    )(own, peer, tiles)
    tiles = tiles.reshape(steps * blocks, cols // 2, 2 * rows)
    back = lax.all_to_all(tiles, ("gy", "gx"), 0, 0, tiled=True)
    return pl.pallas_call(
        post_kernel,
        out_shape=jax.ShapeDtypeStruct((rows, cols, width), jnp.bfloat16),
        in_specs=[VMEM] * 6,
        out_specs=VMEM,
        compiler_params=PARAMS,
        scratch_shapes=[
            pltpu.VMEM((hidden * cols // 2, 2 * rows), jnp.float32),
            pltpu.VMEM((rows * cols, width), jnp.float32),
        ],
        name="post",
    )(back.reshape(hidden // 2, cols, 2 * rows), normed, w_gate, out_gain[None], out_bias[None], w_out)


def solution(mesh):
    in_specs = (P(("grp", "gx", "gz"), "gy", None), P("grp"), P(), P(), P(), P(), P(), P(), P())
    out_specs = P(("grp", "gx", "gz"), "gy", None)
    return jax.shard_map(body, mesh=mesh, in_specs=in_specs, out_specs=out_specs, check_vma=False)
```

time: 179 us -> 174 us (0.972)
  blocking collectives: 113 us -> 163 us
  waiting for transfers between devices: 41.4 us -> 1.37 us
  starting transfers between devices: 12 us -> 1.94 us
  Pallas kernels: 8.18 us -> 3.59 us
    all_to_all x0 -> x1, blocking collectives: none -> 50.3 us  [body(): back = lax.all_to_all(tiles, ('gy', 'gx'), 0, 0, tiled=True)]
    all_to_all x1 -> x0, waiting for transfers between devices: 39.5 us -> none  [body(): back = lax.all_to_all(tiles, ('gy', 'gx'), 0, 0, tiled=True)]
    all_to_all x1 -> x0, starting transfers between devices: 10 us -> none  [body(): back = lax.all_to_all(tiles, ('gy', 'gx'), 0, 0, tiled=True)]
    pallas_call x1, Pallas kernels: 3.11 us -> 1.29 us  [body(): pl.pallas_call(pre_kernel, out_shape=(jax.ShapeDtypeStruct((rows * cols,...]
  transfers between devices with their start and end apart: 2 -> 1, of which waited for: 2 -> 1; matrix products, arithmetic and copies ran while one was open for 1% -> 0% of each run, Pallas kernels for 0% -> 0%
where the time goes in v2:
time: 174 us
  blocking collectives  163 us (94%)
  Pallas kernels  3.59 us (2%)
  local copies, waits for them, and re-layouts  3.18 us (2%)
  starting transfers between devices  1.94 us (1%)
    all_to_all x1, blocking collectives, body(): own = lax.all_to_all(operands, ('gy', 'gx'), 0, 0, tiled=True)  113 us
    all_to_all x1, blocking collectives, body(): back = lax.all_to_all(tiles, ('gy', 'gx'), 0, 0, tiled=True)  50.3 us
  transfers between devices with their start and end apart: 1, of which 1 were waited for; matrix products, arithmetic and copies ran while one was open for 0% of the time, Pallas kernels for 0%

profile of v2, /device:TPU:38, one launch (start us, length us, event | category | flops | bytes accessed | tf_op | source)
XLA Modules:
  0.0 173.6 jit_solution(9206909181298436152)
XLA Ops:
  0.7 0.0 copy-start.4
  0.7 0.0 copy-start.5
  0.7 0.6 copy-done.4
  1.3 0.0 copy-done.5
  1.3 0.0 copy-start
  1.3 0.9 copy-done
  2.3 0.0 copy-start.1
  2.3 0.9 copy-done.1
  3.2 1.3 pre.1
  4.5 112.5 %all_to_all.10 = bf16[128,16,128]{2,1,0:T(8,128)(2,1)S(1)} all-to-all(bf16[128,16,128]{2,1,0:T(8,128)(2,1)S(1)} %get-tuple-element.7), channel_id=1, replica_groups=mesh['grp'=2,'gy'=32,'gx'=4,'gz'=2] {'gy','gx'}, dimensions={0} | all-to-all | bytes 1048576 | tf_op jit(solution)/shard_map/all_to_all | solution.py:138
  117.0 1.9 %collective-permute-start = (bf16[128,16,128]{2,1,0:T(8,128)(2,1)S(1)}, bf16[128,16,128]{2,1,0:T(8,128)(2,1)S(1)}, u32[]{:S(2)}, u32[]{:S(2)}) collective-permute-start(bf16[128,16,128]{2,1,0:T(8,128)(2,1)S(1)} %all_to_all.10), channel_id=1, source_target_pairs={{0,1},{1,0},{2,3},{3,2},{4,5},{5,4},{6,7},{7,6},{8,9},{9,8},{10,11... | collective-permute-start | bytes 1572872 | tf_op jit(solution)/shard_map/ppermute | solution.py:139
  119.0 0.5 own.1.done_ref
  119.5 1.4 collective-permute-done
  120.8 0.5 peer.1
  121.3 0.0 copy-start.2
  121.4 0.0 copy-start.3
  121.4 50.3 %all_to_all.11 = bf16[128,8,128]{2,1,0:T(8,128)(2,1)S(1)} all-to-all(bf16[128,8,128]{2,1,0:T(8,128)(2,1)S(1)} %bitcast.10), channel_id=1, replica_groups=mesh['grp'=2,'gy'=32,'gx'=4,'gz'=2] {'gy','gx'}, dimensions={0} | all-to-all | bytes 524288 | tf_op jit(solution)/shard_map/all_to_all | solution.py:161
  171.7 0.0 copy-start.6
  171.7 0.0 copy-start.7
  171.7 0.0 copy-done.2
  171.7 0.0 copy-done.3
  171.7 0.6 copy-done.6
  172.3 0.0 copy-done.7
  172.3 1.3 post.1
Async XLA Ops:
  0.7 0.7 copy-start.4
  0.7 0.7 copy-start.5
  1.3 0.9 copy-start
  2.3 0.9 copy-start.1
  117.0 3.8 %collective-permute-start = (bf16[128,16,128]{2,1,0:T(8,128)(2,1)S(1)}, bf16[128,16,128]{2,1,0:T(8,128)(2,1)S(1)}, u32[]{:S(2)}, u32[]{:S(2)}) collective-permute-start(bf16[128,16,128]{2,1,0:T(8,128)(2,1)S(1)} %all_to_all.10), channel_id=1, source_target_pairs={{0,1},{1,0},{2,3},{3,2},{4,5},{5,4},{6,7},{7,6},{8,9},{9,8},{10,11... | collective-permute-start | bytes 1572872 | tf_op jit(solution)/shard_map/ppermute | solution.py:139
  121.3 50.3 %copy-start.2 = (bf16[128,128]{1,0:T(8,128)(2,1)S(1)}, bf16[128,128]{1,0:T(8,128)(2,1)}, u32[]{:S(2)}) copy-start(bf16[128,128]{1,0:T(8,128)(2,1)} %w_gate.1) | copy-start | bytes 98308
  121.4 50.3 %copy-start.3 = (bf16[128,128]{1,0:T(8,128)(2,1)S(1)}, bf16[128,128]{1,0:T(8,128)(2,1)}, u32[]{:S(2)}) copy-start(bf16[128,128]{1,0:T(8,128)(2,1)} %w_ref.3) | copy-start | bytes 98308
  171.7 0.7 copy-start.6
  171.7 0.7 copy-start.7

commit v3 on v2

--- a/solution.py
+++ b/solution.py
@@ -20,14 +20,17 @@
     return pltpu.roll(value, value.shape[-1] // 2, value.ndim - 1)
 
 
+def center_kernel(x_ref, out_ref):
+    x = x_ref[...].reshape(out_ref.shape).astype(jnp.float32)
+    x = x - jnp.mean(x, -1, keepdims=True)
+    spread = jnp.mean(x * x, -1, keepdims=True)
+    out_ref[...] = x * lax.rsqrt(spread + EPS)
+
+
 def pre_kernel(length, x_ref, gain, bias, w_ref, normed_ref, out_ref, rows_s, out_s):
-    rows, cols, width = x_ref.shape
-    hidden = w_ref.shape[1] // 4
-    x = x_ref[...].reshape(rows * cols, width).astype(jnp.float32)
-    mean = jnp.mean(x, -1, keepdims=True)
-    x = x - mean
-    spread = jnp.mean(x * x, -1, keepdims=True)
-    normed = (x * lax.rsqrt(spread + EPS) * gain[...] + bias[...]).astype(jnp.bfloat16)
+    hidden, cols, rows = out_ref.shape
+    rows = rows // 2
+    normed = (x_ref[...] * gain[...] + bias[...]).astype(jnp.bfloat16)
     normed_ref[...] = normed
     rows_s[...] = normed.astype(jnp.float32)
     w_t = w_ref[...].astype(jnp.float32).T.astype(jnp.bfloat16)
@@ -75,11 +78,14 @@
     return [t.reshape(blocks, t.shape[0] // blocks, depth, lanes) for t in tiles]
 
 
-def own_kernel(own_ref, out_ref):
+def own_kernel(own_ref, normed, w_gate, gain, bias, out_ref, gate_ref, gain_t, bias_t):
     half = own_ref.shape[3] // 2
     tiles = product(operand(own_ref, 0), operand(own_ref, half), own_ref.shape[2])
     for pair, tile in enumerate(tiles):
         out_ref[:, :, pair] = tile
+    gate_ref[...] = jax.nn.sigmoid(jnp.dot(normed[...], w_gate[...], preferred_element_type=jnp.float32))
+    gain_t[...] = jnp.broadcast_to(gain[...], gain_t.shape[::-1]).T
+    bias_t[...] = jnp.broadcast_to(bias[...], bias_t.shape[::-1]).T
 
 
 def peer_kernel(own_ref, peer_ref, done_ref, out_ref):
@@ -91,28 +97,42 @@
         out_ref[:, 1 - core, :, pair] = tile
 
 
-def post_kernel(t_ref, normed, w_gate, gain, bias, w_ref, out_ref, t_s, out_s):
-    rows, cols, width = out_ref.shape
+def post_kernel(t_ref, gate, gain_t, bias_t, w_ref, out_hbm, t_s, out_s, out_v, sems):
+    rows, cols, width = out_v.shape
     hidden = w_ref.shape[0]
     depth = cols // 2
     t_s[...] = t_ref[...].astype(jnp.float32).reshape(t_s.shape)
-    gain_t = jnp.broadcast_to(gain[...], (2 * rows, hidden)).T
-    bias_t = jnp.broadcast_to(bias[...], (2 * rows, hidden)).T
     w = w_ref[...]
     for r in range(depth):
         t = t_s[pl.ds(r, hidden, stride=depth), :]
         t = t - jnp.mean(t, 0, keepdims=True)
         spread = jnp.mean(t * t, 0, keepdims=True)
-        t = (t * lax.rsqrt(spread + EPS) * gain_t + bias_t).astype(jnp.bfloat16)
+        t = (t * lax.rsqrt(spread + EPS) * gain_t[...] + bias_t[...]).astype(jnp.bfloat16)
         o = lax.dot_general(t, w, TN, preferred_element_type=jnp.float32)
         out_s[pl.ds(r, rows, stride=cols), :] = o[:rows]
         out_s[pl.ds(depth + r, rows, stride=cols), :] = o[rows:]
-    gate = jax.nn.sigmoid(jnp.dot(normed[...], w_gate[...], preferred_element_type=jnp.float32))
-    out_ref[...] = (gate * out_s[...]).astype(jnp.bfloat16).reshape(out_ref.shape)
+    parts = sems.shape[0]
+    step = rows // parts
+    copies = []
+    for p in range(parts):
+        here = pl.ds(p * step * cols, step * cols)
+        out_v[pl.ds(p * step, step)] = (
+            (gate[here] * out_s[here]).astype(jnp.bfloat16).reshape(step, cols, width)
+        )
+        copies.append(
+            pltpu.make_async_copy(
+                out_v.at[pl.ds(p * step, step)], out_hbm.at[pl.ds(p * step, step)], sems.at[p]
+            )
+        )
+        copies[-1].start()
+    for copy in copies:
+        copy.wait()
 
 
 SMEM = pl.BlockSpec(memory_space=pltpu.SMEM)
 VMEM = pl.BlockSpec(memory_space=pltpu.VMEM)
+HBM = pl.BlockSpec(memory_space=pltpu.HBM)
+COST = pl.CostEstimate(flops=2**30, bytes_accessed=2**20, transcendentals=0)
 PARAMS = pltpu.CompilerParams(vmem_limit_bytes=16 * 2**20)
 
 
@@ -120,41 +140,59 @@
     rows, cols, width = pair.shape
     hidden = w_out.shape[0]
     steps, blocks, cores = (lax.axis_size(a) for a in ("gy", "gx", "gz"))
+    parts = 4
+    flat, square = (rows * cols, width), (hidden, 2 * rows)
+    centered = pl.pallas_call(
+        center_kernel,
+        out_shape=jax.ShapeDtypeStruct(flat, jnp.float32),
+        in_specs=[VMEM],
+        out_specs=VMEM,
+        compiler_params=PARAMS,
+        cost_estimate=COST,
+        name="center",
+    )(pair)
     normed, operands = pl.pallas_call(
         pre_kernel,
         out_shape=(
-            jax.ShapeDtypeStruct((rows * cols, width), jnp.bfloat16),
+            jax.ShapeDtypeStruct(flat, jnp.bfloat16),
             jax.ShapeDtypeStruct((hidden, cols, 2 * rows), jnp.bfloat16),
         ),
-        in_specs=[SMEM, VMEM, VMEM, VMEM, VMEM],
-        compiler_params=PARAMS,
+        in_specs=[SMEM] + [VMEM] * 4,
         out_specs=(VMEM, VMEM),
         scratch_shapes=[
-            pltpu.VMEM((rows * cols, width), jnp.float32),
+            pltpu.VMEM(flat, jnp.float32),
             pltpu.VMEM((hidden * cols, 2 * rows), jnp.float32),
         ],
+        compiler_params=PARAMS,
+        cost_estimate=COST,
         name="pre",
-    )(lengths, pair, ln_gain[None], ln_bias[None], w_ab)
+    )(lengths, centered, ln_gain[None], ln_bias[None], w_ab)
     own = lax.all_to_all(operands, ("gy", "gx"), 0, 0, tiled=True)
     peer = lax.ppermute(own, "gz", [(g, cores - 1 - g) for g in range(cores)])
     shape = (steps, blocks, cols, 2 * rows)
     own, peer = own.reshape(shape), peer.reshape(shape)
     group = (blocks, rows // cols, blocks // 2, cols, 2 * rows)
-    tiles = pl.pallas_call(
+    tiles, gate, gain_t, bias_t = pl.pallas_call(
         own_kernel,
-        out_shape=jax.ShapeDtypeStruct(group, jnp.bfloat16),
-        in_specs=[VMEM],
-        out_specs=VMEM,
-        compiler_params=PARAMS,
-        cost_estimate=pl.CostEstimate(flops=2**30, bytes_accessed=2**20, transcendentals=0),
+        out_shape=(
+            jax.ShapeDtypeStruct(group, jnp.bfloat16),
+            jax.ShapeDtypeStruct(flat, jnp.float32),
+            jax.ShapeDtypeStruct(square, jnp.float32),
+            jax.ShapeDtypeStruct(square, jnp.float32),
+        ),
+        in_specs=[VMEM] * 5,
+        out_specs=(VMEM,) * 4,
+        compiler_params=PARAMS,
+        cost_estimate=COST,
         name="own",
-    )(own)
+    )(own, normed, w_gate, out_gain[None], out_bias[None])
     tiles = pl.pallas_call(
         peer_kernel,
         out_shape=jax.ShapeDtypeStruct((blocks, cores, *group[1:]), jnp.bfloat16),
         in_specs=[VMEM] * 3,
         out_specs=VMEM,
         compiler_params=PARAMS,
+        cost_estimate=COST,
         name="peer",
     )(own, peer, tiles)
     tiles = tiles.reshape(steps * blocks, cols // 2, 2 * rows)
@@ -162,15 +200,17 @@
     return pl.pallas_call(
         post_kernel,
         out_shape=jax.ShapeDtypeStruct((rows, cols, width), jnp.bfloat16),
-        in_specs=[VMEM] * 6,
-        out_specs=VMEM,
-        compiler_params=PARAMS,
+        in_specs=[VMEM] * 5,
+        out_specs=HBM,
         scratch_shapes=[
             pltpu.VMEM((hidden * cols // 2, 2 * rows), jnp.float32),
-            pltpu.VMEM((rows * cols, width), jnp.float32),
+            pltpu.VMEM(flat, jnp.float32),
+            pltpu.VMEM((rows, cols, width), jnp.bfloat16),
+            pltpu.SemaphoreType.DMA((parts,)),
         ],
+        compiler_params=PARAMS,
         name="post",
-    )(back.reshape(hidden // 2, cols, 2 * rows), normed, w_gate, out_gain[None], out_bias[None], w_out)
+    )(back.reshape(hidden // 2, cols, 2 * rows), gate, gain_t, bias_t, w_out)
 
 
 def solution(mesh):

time: 174 us -> 172 us (0.989)
  no operation moved by 1% of the time
where the time goes in v3:
time: 172 us
  blocking collectives  163 us (95%)
  Pallas kernels  3.57 us (2%)
  local copies, waits for them, and re-layouts  2.28 us (1%)
  starting transfers between devices  1.94 us (1%)
    all_to_all x1, blocking collectives, body(): own = lax.all_to_all(operands, ('gy', 'gx'), 0, 0, tiled=True)  113 us
    all_to_all x1, blocking collectives, body(): back = lax.all_to_all(tiles, ('gy', 'gx'), 0, 0, tiled=True)  50.3 us
  transfers between devices with their start and end apart: 1, of which 1 were waited for; matrix products, arithmetic and copies ran while one was open for 0% of the time, Pallas kernels for 0%

profile of v3, /device:TPU:38, one launch (start us, length us, event | category | flops | bytes accessed | tf_op | source)
XLA Modules:
  0.0 172.0 jit_solution(13820482472954734740)
XLA Ops:
  0.7 0.0 copy-start.1
  0.7 0.9 copy-done.1
  1.6 0.0 copy-start.2
  1.6 0.3 center.1.x_ref
  2.0 0.0 copy-start.4
  2.0 0.0 copy-start.5
  2.0 0.5 copy-done.2
  2.5 0.1 copy-done.4
  2.6 0.0 copy-done.5
  2.7 0.9 pre.1
  3.5 0.0 copy-start.3
  3.5 112.5 %all_to_all.10 = bf16[128,16,128]{2,1,0:T(8,128)(2,1)S(1)} all-to-all(bf16[128,16,128]{2,1,0:T(8,128)(2,1)S(1)} %get-tuple-element.11), channel_id=1, replica_groups=mesh['grp'=2,'gy'=32,'gx'=4,'gz'=2] {'gy','gx'}, dimensions={0} | all-to-all | bytes 1048576 | tf_op jit(solution)/shard_map/all_to_all | solution.py:170
  116.1 1.9 %collective-permute-start = (bf16[128,16,128]{2,1,0:T(8,128)(2,1)S(1)}, bf16[128,16,128]{2,1,0:T(8,128)(2,1)S(1)}, u32[]{:S(2)}, u32[]{:S(2)}) collective-permute-start(bf16[128,16,128]{2,1,0:T(8,128)(2,1)S(1)} %all_to_all.10), channel_id=1, source_target_pairs={{0,1},{1,0},{2,3},{3,2},{4,5},{5,4},{6,7},{7,6},{8,9},{9,8},{10,11... | collective-permute-start | bytes 1572872 | tf_op jit(solution)/shard_map/ppermute | solution.py:171
  118.0 0.0 copy-start.6
  118.0 0.0 copy-start.7
  118.0 0.0 copy-done.3
  118.0 0.6 copy-done.6
  118.7 0.0 copy-done.7
  118.7 0.6 own.1
  119.3 0.6 collective-permute-done
  119.9 0.5 peer.1
  120.4 0.0 copy-start
  120.4 50.3 %all_to_all.11 = bf16[128,8,128]{2,1,0:T(8,128)(2,1)S(1)} all-to-all(bf16[128,8,128]{2,1,0:T(8,128)(2,1)S(1)} %bitcast.11), channel_id=1, replica_groups=mesh['grp'=2,'gy'=32,'gx'=4,'gz'=2] {'gy','gx'}, dimensions={0} | all-to-all | bytes 524288 | tf_op jit(solution)/shard_map/all_to_all | solution.py:199
  170.7 0.0 copy-done
  170.7 1.3 post.1
Async XLA Ops:
  0.7 1.0 copy-start.1
  1.6 0.9 copy-start.2
  2.0 0.7 copy-start.4
  2.0 0.7 copy-start.5
  3.5 114.5 %copy-start.3 = (bf16[128,128]{1,0:T(8,128)(2,1)S(1)}, bf16[128,128]{1,0:T(8,128)(2,1)}, u32[]{:S(2)}) copy-start(bf16[128,128]{1,0:T(8,128)(2,1)} %w_gate.1) | copy-start | bytes 98308
  116.1 3.8 %collective-permute-start = (bf16[128,16,128]{2,1,0:T(8,128)(2,1)S(1)}, bf16[128,16,128]{2,1,0:T(8,128)(2,1)S(1)}, u32[]{:S(2)}, u32[]{:S(2)}) collective-permute-start(bf16[128,16,128]{2,1,0:T(8,128)(2,1)S(1)} %all_to_all.10), channel_id=1, source_target_pairs={{0,1},{1,0},{2,3},{3,2},{4,5},{5,4},{6,7},{7,6},{8,9},{9,8},{10,11... | collective-permute-start | bytes 1572872 | tf_op jit(solution)/shard_map/ppermute | solution.py:171
  118.0 0.7 copy-start.6
  118.0 0.7 copy-start.7
  120.4 50.3 %copy-start = (bf16[128,128]{1,0:T(8,128)(2,1)S(1)}, bf16[128,128]{1,0:T(8,128)(2,1)}, u32[]{:S(2)}) copy-start(bf16[128,128]{1,0:T(8,128)(2,1)} %w_ref.3) | copy-start | bytes 98308

commit v4 on v3

--- a/solution.py
+++ b/solution.py
@@ -20,32 +20,31 @@
     return pltpu.roll(value, value.shape[-1] // 2, value.ndim - 1)
 
 
-def center_kernel(x_ref, out_ref):
-    x = x_ref[...].reshape(out_ref.shape).astype(jnp.float32)
+def center_kernel(x_ref, out_ref, rows_s):
+    cols, rows, width = out_ref.shape
+    x = x_ref[...].reshape(rows * cols, width).astype(jnp.float32)
     x = x - jnp.mean(x, -1, keepdims=True)
     spread = jnp.mean(x * x, -1, keepdims=True)
-    out_ref[...] = x * lax.rsqrt(spread + EPS)
-
-
-def pre_kernel(length, x_ref, gain, bias, w_ref, normed_ref, out_ref, rows_s, out_s):
-    hidden, cols, rows = out_ref.shape
-    rows = rows // 2
-    normed = (x_ref[...] * gain[...] + bias[...]).astype(jnp.bfloat16)
-    normed_ref[...] = normed
-    rows_s[...] = normed.astype(jnp.float32)
+    rows_s[...] = x * lax.rsqrt(spread + EPS)
+    for k in range(cols):
+        out_ref[k] = rows_s[pl.ds(k, rows, stride=cols), :]
+
+
+def pre_kernel(length, x_ref, gain, bias, w_ref, normed_ref, out_ref, out_s):
+    cols, rows, width = x_ref.shape
+    hidden = out_ref.shape[0]
     w_t = w_ref[...].astype(jnp.float32).T.astype(jnp.bfloat16)
     low = low_half((1, 2 * rows))
     lane = lax.broadcasted_iota(jnp.int32, (1, 2 * rows), 1)
     row_start = (lax.axis_index("gx") * lax.axis_size("gz") + lax.axis_index("gz")) * rows
     col_start = lax.axis_index("gy") * cols
-    row_live = row_start + jnp.where(low, lane, lane - rows) < length[0]
-    for pair in range(cols // 2):
-        k = 2 * pair
-        block = jnp.concatenate(
-            [rows_s[pl.ds(k, rows, stride=cols), :], rows_s[pl.ds(k + 1, rows, stride=cols), :]], 0
-        ).astype(jnp.bfloat16)
+    row_live = row_start + jnp.where(low, lane, lane - rows) < length[...]
+    for k in range(0, cols, 2):
+        block = x_ref[pl.ds(k, 2)].reshape(2 * rows, width)
+        block = (block * gain[...] + bias[...]).astype(jnp.bfloat16)
+        normed_ref[pl.ds(k * rows, 2 * rows)] = block
         proj = lax.dot_general(w_t, block, NT, preferred_element_type=jnp.float32)
-        col_live = col_start + k + jnp.where(low, 0, 1) < length[0]
+        col_live = col_start + k + jnp.where(low, 0, 1) < length[...]
         mask = jnp.where(row_live & col_live, 1.0, 0.0)
         left = mask * jax.nn.sigmoid(proj[:hidden]) * proj[hidden : 2 * hidden]
         right = mask * jax.nn.sigmoid(proj[2 * hidden : 3 * hidden]) * proj[3 * hidden :]
@@ -109,15 +108,16 @@
         spread = jnp.mean(t * t, 0, keepdims=True)
         t = (t * lax.rsqrt(spread + EPS) * gain_t[...] + bias_t[...]).astype(jnp.bfloat16)
         o = lax.dot_general(t, w, TN, preferred_element_type=jnp.float32)
-        out_s[pl.ds(r, rows, stride=cols), :] = o[:rows]
-        out_s[pl.ds(depth + r, rows, stride=cols), :] = o[rows:]
+        for half, col in enumerate((r, depth + r)):
+            here = slice(half * rows, (half + 1) * rows)
+            out_s[pl.ds(col, rows, stride=cols), :] = gate[pl.ds(col * rows, rows)] * o[here]
     parts = sems.shape[0]
     step = rows // parts
     copies = []
     for p in range(parts):
         here = pl.ds(p * step * cols, step * cols)
         out_v[pl.ds(p * step, step)] = (
-            (gate[here] * out_s[here]).astype(jnp.bfloat16).reshape(step, cols, width)
+            out_s[here].astype(jnp.bfloat16).reshape(step, cols, width)
         )
         copies.append(
             pltpu.make_async_copy(
@@ -129,7 +129,6 @@
         copy.wait()
 
 
-SMEM = pl.BlockSpec(memory_space=pltpu.SMEM)
 VMEM = pl.BlockSpec(memory_space=pltpu.VMEM)
 HBM = pl.BlockSpec(memory_space=pltpu.HBM)
 COST = pl.CostEstimate(flops=2**30, bytes_accessed=2**20, transcendentals=0)
@@ -144,9 +143,10 @@
     flat, square = (rows * cols, width), (hidden, 2 * rows)
     centered = pl.pallas_call(
         center_kernel,
-        out_shape=jax.ShapeDtypeStruct(flat, jnp.float32),
+        out_shape=jax.ShapeDtypeStruct((cols, rows, width), jnp.float32),
         in_specs=[VMEM],
         out_specs=VMEM,
+        scratch_shapes=[pltpu.VMEM(flat, jnp.float32)],
         compiler_params=PARAMS,
         cost_estimate=COST,
         name="center",
@@ -157,16 +157,13 @@
             jax.ShapeDtypeStruct(flat, jnp.bfloat16),
             jax.ShapeDtypeStruct((hidden, cols, 2 * rows), jnp.bfloat16),
         ),
-        in_specs=[SMEM] + [VMEM] * 4,
+        in_specs=[VMEM] * 5,
         out_specs=(VMEM, VMEM),
-        scratch_shapes=[
-            pltpu.VMEM(flat, jnp.float32),
-            pltpu.VMEM((hidden * cols, 2 * rows), jnp.float32),
-        ],
+        scratch_shapes=[pltpu.VMEM((hidden * cols, 2 * rows), jnp.float32)],
         compiler_params=PARAMS,
         cost_estimate=COST,
         name="pre",
-    )(lengths, centered, ln_gain[None], ln_bias[None], w_ab)
+    )(lengths[None], centered, ln_gain[None], ln_bias[None], w_ab)
     own = lax.all_to_all(operands, ("gy", "gx"), 0, 0, tiled=True)
     peer = lax.ppermute(own, "gz", [(g, cores - 1 - g) for g in range(cores)])
     shape = (steps, blocks, cols, 2 * rows)

time: 172 us -> 172 us (level)
  no operation moved by 1% of the time
where the time goes in v4:
time: 172 us
  blocking collectives  163 us (95%)
  Pallas kernels  3.66 us (2%)
  local copies, waits for them, and re-layouts  2.28 us (1%)
  starting transfers between devices  1.94 us (1%)
    all_to_all x1, blocking collectives, body(): own = lax.all_to_all(operands, ('gy', 'gx'), 0, 0, tiled=True)  113 us
    all_to_all x1, blocking collectives, body(): back = lax.all_to_all(tiles, ('gy', 'gx'), 0, 0, tiled=True)  50.3 us
  transfers between devices with their start and end apart: 1, of which 1 were waited for; matrix products, arithmetic and copies ran while one was open for 0% of the time, Pallas kernels for 0%

profile of v4, /device:TPU:38, one launch (start us, length us, event | category | flops | bytes accessed | tf_op | source)
XLA Modules:
  0.0 172.1 jit_solution(5552375388418342672)
XLA Ops:
  0.7 0.0 copy-start.1
  0.7 0.9 copy-done.1
  1.6 0.0 copy-start.2
  1.6 0.5 center.1.x_ref
  2.1 0.0 copy-start.4
  2.1 0.0 copy-start.5
  2.1 0.4 copy-done.2
  2.5 0.3 copy-done.4
  2.8 0.0 copy-done.5
  2.8 0.8 pre.1
  3.6 0.0 copy-start.3
  3.6 112.5 %all_to_all.10 = bf16[128,16,128]{2,1,0:T(8,128)(2,1)S(1)} all-to-all(bf16[128,16,128]{2,1,0:T(8,128)(2,1)S(1)} %get-tuple-element.11), channel_id=1, replica_groups=mesh['grp'=2,'gy'=32,'gx'=4,'gz'=2] {'gy','gx'}, dimensions={0} | all-to-all | bytes 1048576 | tf_op jit(solution)/shard_map/all_to_all | solution.py:167
  116.1 1.9 %collective-permute-start = (bf16[128,16,128]{2,1,0:T(8,128)(2,1)S(1)}, bf16[128,16,128]{2,1,0:T(8,128)(2,1)S(1)}, u32[]{:S(2)}, u32[]{:S(2)}) collective-permute-start(bf16[128,16,128]{2,1,0:T(8,128)(2,1)S(1)} %all_to_all.10), channel_id=1, source_target_pairs={{0,1},{1,0},{2,3},{3,2},{4,5},{5,4},{6,7},{7,6},{8,9},{9,8},{10,11... | collective-permute-start | bytes 1572872 | tf_op jit(solution)/shard_map/ppermute | solution.py:168
  118.1 0.0 copy-start.6
  118.1 0.0 copy-start.7
  118.1 0.0 copy-done.3
  118.1 0.6 copy-done.6
  118.7 0.0 copy-done.7
  118.8 0.6 own.1
  119.4 0.6 collective-permute-done
  120.0 0.5 peer.1
  120.5 0.0 copy-start
  120.5 50.3 %all_to_all.11 = bf16[128,8,128]{2,1,0:T(8,128)(2,1)S(1)} all-to-all(bf16[128,8,128]{2,1,0:T(8,128)(2,1)S(1)} %bitcast.13), channel_id=1, replica_groups=mesh['grp'=2,'gy'=32,'gx'=4,'gz'=2] {'gy','gx'}, dimensions={0} | all-to-all | bytes 524288 | tf_op jit(solution)/shard_map/all_to_all | solution.py:196
  170.8 0.0 copy-done
  170.8 1.3 post.1
Async XLA Ops:
  0.7 1.0 copy-start.1
  1.6 0.9 copy-start.2
  2.1 0.7 copy-start.4
  2.1 0.7 copy-start.5
  3.6 114.5 %copy-start.3 = (bf16[128,128]{1,0:T(8,128)(2,1)S(1)}, bf16[128,128]{1,0:T(8,128)(2,1)}, u32[]{:S(2)}) copy-start(bf16[128,128]{1,0:T(8,128)(2,1)} %w_gate.1) | copy-start | bytes 98308
  116.1 3.8 %collective-permute-start = (bf16[128,16,128]{2,1,0:T(8,128)(2,1)S(1)}, bf16[128,16,128]{2,1,0:T(8,128)(2,1)S(1)}, u32[]{:S(2)}, u32[]{:S(2)}) collective-permute-start(bf16[128,16,128]{2,1,0:T(8,128)(2,1)S(1)} %all_to_all.10), channel_id=1, source_target_pairs={{0,1},{1,0},{2,3},{3,2},{4,5},{5,4},{6,7},{7,6},{8,9},{9,8},{10,11... | collective-permute-start | bytes 1572872 | tf_op jit(solution)/shard_map/ppermute | solution.py:168
  118.1 0.7 copy-start.6
  118.1 0.7 copy-start.7
  120.5 50.3 %copy-start = (bf16[128,128]{1,0:T(8,128)(2,1)S(1)}, bf16[128,128]{1,0:T(8,128)(2,1)}, u32[]{:S(2)}) copy-start(bf16[128,128]{1,0:T(8,128)(2,1)} %w_ref.3) | copy-start | bytes 98308

commit v5 on v4

--- a/solution.py
+++ b/solution.py
@@ -30,34 +30,33 @@
         out_ref[k] = rows_s[pl.ds(k, rows, stride=cols), :]
 
 
-def pre_kernel(length, x_ref, gain, bias, w_ref, normed_ref, out_ref, out_s):
+def pre_kernel(x_ref, gain, bias, w_ref, normed_ref, out_ref, out_s):
     cols, rows, width = x_ref.shape
     hidden = out_ref.shape[0]
     w_t = w_ref[...].astype(jnp.float32).T.astype(jnp.bfloat16)
     low = low_half((1, 2 * rows))
-    lane = lax.broadcasted_iota(jnp.int32, (1, 2 * rows), 1)
-    row_start = (lax.axis_index("gx") * lax.axis_size("gz") + lax.axis_index("gz")) * rows
-    col_start = lax.axis_index("gy") * cols
-    row_live = row_start + jnp.where(low, lane, lane - rows) < length[...]
     for k in range(0, cols, 2):
         block = x_ref[pl.ds(k, 2)].reshape(2 * rows, width)
         block = (block * gain[...] + bias[...]).astype(jnp.bfloat16)
         normed_ref[pl.ds(k * rows, 2 * rows)] = block
         proj = lax.dot_general(w_t, block, NT, preferred_element_type=jnp.float32)
-        col_live = col_start + k + jnp.where(low, 0, 1) < length[...]
-        mask = jnp.where(row_live & col_live, 1.0, 0.0)
-        left = mask * jax.nn.sigmoid(proj[:hidden]) * proj[hidden : 2 * hidden]
-        right = mask * jax.nn.sigmoid(proj[2 * hidden : 3 * hidden]) * proj[3 * hidden :]
+        left = jax.nn.sigmoid(proj[:hidden]) * proj[hidden : 2 * hidden]
+        right = jax.nn.sigmoid(proj[2 * hidden : 3 * hidden]) * proj[3 * hidden :]
         out_s[pl.ds(k, hidden, stride=cols), :] = jnp.where(low, left, swap_halves(right))
         out_s[pl.ds(k + 1, hidden, stride=cols), :] = jnp.where(low, swap_halves(left), right)
     out_ref[...] = out_s[...].astype(jnp.bfloat16).reshape(out_ref.shape)
 
 
-def operand(ref, first):
+def operand(ref, first, length, core, mask_k):
     steps, blocks, depth, lanes = ref.shape
     half = lanes // 2
     parts = [ref[:, x].reshape(steps * depth, lanes)[:, first : first + half] for x in range(blocks)]
-    return jnp.concatenate(parts, 1)
+    value = jnp.concatenate(parts, 1)
+    lane = lax.broadcasted_iota(jnp.int32, (1, blocks * half), 1)
+    live = lane // half * (lax.axis_size("gz") * half) + core * half + lane % half < length
+    if mask_k:
+        live = live & (lax.broadcasted_iota(jnp.int32, (steps * depth, 1), 0) < length)
+    return value * jnp.where(live, 1.0, 0.0).astype(jnp.bfloat16)
 
 
 def product(left, right, depth):
@@ -77,9 +76,12 @@
     return [t.reshape(blocks, t.shape[0] // blocks, depth, lanes) for t in tiles]
 
 
-def own_kernel(own_ref, normed, w_gate, gain, bias, out_ref, gate_ref, gain_t, bias_t):
+def own_kernel(length, own_ref, normed, w_gate, gain, bias, out_ref, left_ref, gate_ref, gain_t, bias_t):
     half = own_ref.shape[3] // 2
-    tiles = product(operand(own_ref, 0), operand(own_ref, half), own_ref.shape[2])
+    core = lax.axis_index("gz")
+    left = operand(own_ref, 0, length[0], core, True)
+    left_ref[...] = left
+    tiles = product(left, operand(own_ref, half, length[0], core, False), own_ref.shape[2])
     for pair, tile in enumerate(tiles):
         out_ref[:, :, pair] = tile
     gate_ref[...] = jax.nn.sigmoid(jnp.dot(normed[...], w_gate[...], preferred_element_type=jnp.float32))
@@ -87,12 +89,12 @@
     bias_t[...] = jnp.broadcast_to(bias[...], bias_t.shape[::-1]).T
 
 
-def peer_kernel(own_ref, peer_ref, done_ref, out_ref):
-    half = own_ref.shape[3] // 2
+def peer_kernel(length, left_ref, peer_ref, done_ref, out_ref):
+    half = peer_ref.shape[3] // 2
     core = lax.axis_index("gz")
     out_ref[:, core] = done_ref[...]
-    tiles = product(operand(own_ref, 0), operand(peer_ref, half), own_ref.shape[2])
-    for pair, tile in enumerate(tiles):
+    right = operand(peer_ref, half, length[0], 1 - core, False)
+    for pair, tile in enumerate(product(left_ref[...], right, peer_ref.shape[2])):
         out_ref[:, 1 - core, :, pair] = tile
 
 
@@ -129,6 +131,7 @@
         copy.wait()
 
 
+SMEM = pl.BlockSpec(memory_space=pltpu.SMEM)
 VMEM = pl.BlockSpec(memory_space=pltpu.VMEM)
 HBM = pl.BlockSpec(memory_space=pltpu.HBM)
 COST = pl.CostEstimate(flops=2**30, bytes_accessed=2**20, transcendentals=0)
@@ -157,41 +160,43 @@
             jax.ShapeDtypeStruct(flat, jnp.bfloat16),
             jax.ShapeDtypeStruct((hidden, cols, 2 * rows), jnp.bfloat16),
         ),
-        in_specs=[VMEM] * 5,
+        in_specs=[VMEM] * 4,
         out_specs=(VMEM, VMEM),
         scratch_shapes=[pltpu.VMEM((hidden * cols, 2 * rows), jnp.float32)],
         compiler_params=PARAMS,
         cost_estimate=COST,
         name="pre",
-    )(lengths[None], centered, ln_gain[None], ln_bias[None], w_ab)
+    )(centered, ln_gain[None], ln_bias[None], w_ab)
     own = lax.all_to_all(operands, ("gy", "gx"), 0, 0, tiled=True)
+    own, lengths = lax.optimization_barrier((own, lengths))
     peer = lax.ppermute(own, "gz", [(g, cores - 1 - g) for g in range(cores)])
     shape = (steps, blocks, cols, 2 * rows)
     own, peer = own.reshape(shape), peer.reshape(shape)
     group = (blocks, rows // cols, blocks // 2, cols, 2 * rows)
-    tiles, gate, gain_t, bias_t = pl.pallas_call(
+    tiles, left, gate, gain_t, bias_t = pl.pallas_call(
         own_kernel,
         out_shape=(
             jax.ShapeDtypeStruct(group, jnp.bfloat16),
+            jax.ShapeDtypeStruct((steps * cols, blocks * rows), jnp.bfloat16),
             jax.ShapeDtypeStruct(flat, jnp.float32),
             jax.ShapeDtypeStruct(square, jnp.float32),
             jax.ShapeDtypeStruct(square, jnp.float32),
         ),
-        in_specs=[VMEM] * 5,
-        out_specs=(VMEM,) * 4,
+        in_specs=[SMEM] + [VMEM] * 5,
+        out_specs=(VMEM,) * 5,
         compiler_params=PARAMS,
         cost_estimate=COST,
         name="own",
-    )(own, normed, w_gate, out_gain[None], out_bias[None])
+    )(lengths, own, normed, w_gate, out_gain[None], out_bias[None])
     tiles = pl.pallas_call(
         peer_kernel,
         out_shape=jax.ShapeDtypeStruct((blocks, cores, *group[1:]), jnp.bfloat16),
-        in_specs=[VMEM] * 3,
+        in_specs=[SMEM] + [VMEM] * 3,
         out_specs=VMEM,
         compiler_params=PARAMS,
         cost_estimate=COST,
         name="peer",
-    )(own, peer, tiles)
+    )(lengths, left, peer, tiles)
     tiles = tiles.reshape(steps * blocks, cols // 2, 2 * rows)
     back = lax.all_to_all(tiles, ("gy", "gx"), 0, 0, tiled=True)
     return pl.pallas_call(

time: 172 us -> 172 us (level)
  transfers between devices with their start and end apart: 1 -> 1, of which waited for: 1 -> 0; matrix products, arithmetic and copies ran while one was open for 0% -> 0% of each run, Pallas kernels for 0% -> 0%
where the time goes in v5:
time: 172 us
  blocking collectives  163 us (95%)
  Pallas kernels  3.59 us (2%)
  local copies, waits for them, and re-layouts  2.28 us (1%)
  starting transfers between devices  1.94 us (1%)
    all_to_all x1, blocking collectives, body(): own = lax.all_to_all(operands, ('gy', 'gx'), 0, 0, tiled=True)  113 us
    all_to_all x1, blocking collectives, body(): back = lax.all_to_all(tiles, ('gy', 'gx'), 0, 0, tiled=True)  50.7 us
  transfers between devices with their start and end apart: 1, of which 0 were waited for; matrix products, arithmetic and copies ran while one was open for 0% of the time, Pallas kernels for 0%

profile of v5, /device:TPU:38, one launch (start us, length us, event | category | flops | bytes accessed | tf_op | source)
XLA Modules:
  0.0 171.8 jit_solution(3249123012703366383)
XLA Ops:
  0.0 0.0 copy-start.1
  0.0 0.9 copy-done.1
  1.0 0.0 copy-start.2
  1.0 0.5 center.1.x_ref
  1.4 0.0 copy-start.4
  1.4 0.0 copy-start.5
  1.5 0.4 copy-done.2
  1.9 0.3 copy-done.4
  2.1 0.0 copy-done.5
  2.1 0.8 pre.1
  2.9 0.0 copy-start.3
  2.9 112.5 %all_to_all.10 = bf16[128,16,128]{2,1,0:T(8,128)(2,1)S(1)} all-to-all(bf16[128,16,128]{2,1,0:T(8,128)(2,1)S(1)} %get-tuple-element.14), channel_id=1, replica_groups=mesh['grp'=2,'gy'=32,'gx'=4,'gz'=2] {'gy','gx'}, dimensions={0} | all-to-all | bytes 1048576 | tf_op jit(solution)/shard_map/all_to_all | solution.py:170
  115.5 1.9 %collective-permute-start = (bf16[128,16,128]{2,1,0:T(8,128)(2,1)S(1)}, bf16[128,16,128]{2,1,0:T(8,128)(2,1)S(1)}, u32[]{:S(2)}, u32[]{:S(2)}) collective-permute-start(bf16[128,16,128]{2,1,0:T(8,128)(2,1)S(1)} %all_to_all.10), channel_id=1, source_target_pairs={{0,1},{1,0},{2,3},{3,2},{4,5},{5,4},{6,7},{7,6},{8,9},{9,8},{10,11... | collective-permute-start | bytes 1572872 | tf_op jit(solution)/shard_map/ppermute | solution.py:172
  118.1 0.0 copy-start.6
  118.1 0.0 copy-start.7
  118.1 0.0 copy-done.3
  118.1 0.6 copy-done.6
  118.7 0.0 copy-done.7
  118.7 0.6 own.1
  119.3 0.0 collective-permute-done
  119.4 0.4 peer.1
  119.8 0.0 copy-start
  119.8 50.7 %all_to_all.11 = bf16[128,8,128]{2,1,0:T(8,128)(2,1)S(1)} all-to-all(bf16[128,8,128]{2,1,0:T(8,128)(2,1)S(1)} %bitcast.10), channel_id=1, replica_groups=mesh['grp'=2,'gy'=32,'gx'=4,'gz'=2] {'gy','gx'}, dimensions={0} | all-to-all | bytes 524288 | tf_op jit(solution)/shard_map/all_to_all | solution.py:201
  170.5 0.0 copy-done
  170.5 1.3 post.1
Async XLA Ops:
  0.0 0.9 copy-start.1
  1.0 0.9 copy-start.2
  1.4 0.7 copy-start.4
  1.4 0.7 copy-start.5
  2.9 115.2 %copy-start.3 = (bf16[128,128]{1,0:T(8,128)(2,1)S(1)}, bf16[128,128]{1,0:T(8,128)(2,1)}, u32[]{:S(2)}) copy-start(bf16[128,128]{1,0:T(8,128)(2,1)} %w_gate.1) | copy-start | bytes 98308
  115.5 3.9 %collective-permute-start = (bf16[128,16,128]{2,1,0:T(8,128)(2,1)S(1)}, bf16[128,16,128]{2,1,0:T(8,128)(2,1)S(1)}, u32[]{:S(2)}, u32[]{:S(2)}) collective-permute-start(bf16[128,16,128]{2,1,0:T(8,128)(2,1)S(1)} %all_to_all.10), channel_id=1, source_target_pairs={{0,1},{1,0},{2,3},{3,2},{4,5},{5,4},{6,7},{7,6},{8,9},{9,8},{10,11... | collective-permute-start | bytes 1572872 | tf_op jit(solution)/shard_map/ppermute | solution.py:172
  118.1 0.7 copy-start.6
  118.1 0.7 copy-start.7
  119.8 50.7 %copy-start = (bf16[128,128]{1,0:T(8,128)(2,1)S(1)}, bf16[128,128]{1,0:T(8,128)(2,1)}, u32[]{:S(2)}) copy-start(bf16[128,128]{1,0:T(8,128)(2,1)} %w_ref.3) | copy-start | bytes 98308

commit v6 on v5

--- a/solution.py
+++ b/solution.py
@@ -47,13 +47,22 @@
     out_ref[...] = out_s[...].astype(jnp.bfloat16).reshape(out_ref.shape)
 
 
-def operand(ref, first, length, core, mask_k):
+def side():
+    return lax.rem(lax.axis_index("gx") + lax.axis_index("gz"), lax.axis_size("gz"))
+
+
+def core_of(group, block):
+    return lax.rem(group + block, lax.axis_size("gz"))
+
+
+def operand(ref, first, length, group, mask_k):
     steps, blocks, depth, lanes = ref.shape
     half = lanes // 2
     parts = [ref[:, x].reshape(steps * depth, lanes)[:, first : first + half] for x in range(blocks)]
     value = jnp.concatenate(parts, 1)
     lane = lax.broadcasted_iota(jnp.int32, (1, blocks * half), 1)
-    live = lane // half * (lax.axis_size("gz") * half) + core * half + lane % half < length
+    block = lane // half
+    live = (block * lax.axis_size("gz") + core_of(group, block)) * half + lane % half < length
     if mask_k:
         live = live & (lax.broadcasted_iota(jnp.int32, (steps * depth, 1), 0) < length)
     return value * jnp.where(live, 1.0, 0.0).astype(jnp.bfloat16)
@@ -78,10 +87,10 @@
 
 def own_kernel(length, own_ref, normed, w_gate, gain, bias, out_ref, left_ref, gate_ref, gain_t, bias_t):
     half = own_ref.shape[3] // 2
-    core = lax.axis_index("gz")
-    left = operand(own_ref, 0, length[0], core, True)
+    group = side()
+    left = operand(own_ref, 0, length[0], group, True)
     left_ref[...] = left
-    tiles = product(left, operand(own_ref, half, length[0], core, False), own_ref.shape[2])
+    tiles = product(left, operand(own_ref, half, length[0], group, False), own_ref.shape[2])
     for pair, tile in enumerate(tiles):
         out_ref[:, :, pair] = tile
     gate_ref[...] = jax.nn.sigmoid(jnp.dot(normed[...], w_gate[...], preferred_element_type=jnp.float32))
@@ -91,11 +100,13 @@
 
 def peer_kernel(length, left_ref, peer_ref, done_ref, out_ref):
     half = peer_ref.shape[3] // 2
-    core = lax.axis_index("gz")
-    out_ref[:, core] = done_ref[...]
-    right = operand(peer_ref, half, length[0], 1 - core, False)
-    for pair, tile in enumerate(product(left_ref[...], right, peer_ref.shape[2])):
-        out_ref[:, 1 - core, :, pair] = tile
+    group = side()
+    right = operand(peer_ref, half, length[0], group + 1, False)
+    tiles = product(left_ref[...], right, peer_ref.shape[2])
+    for block in range(done_ref.shape[0]):
+        out_ref[block, core_of(group, block)] = done_ref[block]
+        for pair, tile in enumerate(tiles):
+            out_ref[block, core_of(group, block + 1), :, pair] = tile[block]
 
 
 def post_kernel(t_ref, gate, gain_t, bias_t, w_ref, out_hbm, t_s, out_s, out_v, sems):
@@ -167,7 +178,16 @@
         cost_estimate=COST,
         name="pre",
     )(centered, ln_gain[None], ln_bias[None], w_ab)
-    own = lax.all_to_all(operands, ("gy", "gx"), 0, 0, tiled=True)
+    groups = [
+        [(z * blocks + x) * cores + (g + x) % cores for z in range(steps) for x in range(blocks)]
+        for g in range(cores)
+    ]
+
+    def exchange(value):
+        axes = ("gy", "gx", "gz")
+        return lax.all_to_all(value, axes, 0, 0, tiled=True, axis_index_groups=groups)
+
+    own = exchange(operands)
     own, lengths = lax.optimization_barrier((own, lengths))
     peer = lax.ppermute(own, "gz", [(g, cores - 1 - g) for g in range(cores)])
     shape = (steps, blocks, cols, 2 * rows)
@@ -198,7 +218,7 @@
         name="peer",
     )(lengths, left, peer, tiles)
     tiles = tiles.reshape(steps * blocks, cols // 2, 2 * rows)
-    back = lax.all_to_all(tiles, ("gy", "gx"), 0, 0, tiled=True)
+    back = exchange(tiles)
     return pl.pallas_call(
         post_kernel,
         out_shape=jax.ShapeDtypeStruct((rows, cols, width), jnp.bfloat16),

time: 172 us -> 173 us (level)
  starting transfers between devices: 1.94 us -> 4.35 us
  blocking collectives: 163 us -> 161 us
    all_to_all x2, blocking collectives: 163 us -> 161 us  [exchange(): lax.all_to_all(value, axes, 0, 0, tiled=True, axis_index_groups=groups)]
    ppermute x1, starting transfers between devices: 1.94 us -> 4.35 us  [body(): peer = lax.ppermute(own, 'gz', [(g, cores - 1 - g) for g in range(cores)])]
where the time goes in v6:
time: 173 us; the launch traced here: 172 us
  blocking collectives  161 us (93%)
  starting transfers between devices  4.35 us (3%)
  Pallas kernels  3.59 us (2%)
  local copies, waits for them, and re-layouts  2.28 us (1%)
    all_to_all x2, blocking collectives, exchange(): lax.all_to_all(value, axes, 0, 0, tiled=True, axis_index_groups=groups)  161 us
    ppermute x1, starting transfers between devices, body(): peer = lax.ppermute(own, 'gz', [(g, cores - 1 - g) for g in range(cores)])  4.35 us
  transfers between devices with their start and end apart: 1, of which 0 were waited for; matrix products, arithmetic and copies ran while one was open for 0% of the time, Pallas kernels for 0%

profile of v6, /device:TPU:38, one launch (start us, length us, event | category | flops | bytes accessed | tf_op | source)
XLA Modules:
  0.0 171.6 jit_solution(7211056074977629157)
XLA Ops:
  0.0 0.0 copy-start.1
  0.0 0.9 copy-done.1
  1.0 0.0 copy-start.2
  1.0 0.5 center.1.x_ref
  1.4 0.0 copy-start.4
  1.4 0.0 copy-start.5
  1.5 0.4 copy-done.2
  1.9 0.3 copy-done.4
  2.1 0.0 copy-done.5
  2.1 0.8 pre.1
  2.9 0.0 copy-start.3
  2.9 110.3 %all_to_all.10 = bf16[128,16,128]{2,1,0:T(8,128)(2,1)S(1)} all-to-all(bf16[128,16,128]{2,1,0:T(8,128)(2,1)S(1)} %get-tuple-element.14), channel_id=1, replica_groups={{0,3,4,7,8,11,12,15,16,19,20,23,24,27,28,31,32,35,36,39,40,43,44,47,48,..., dimensions={0} | all-to-all | bytes 1048576 | tf_op jit(solution)/shard_map/all_to_all | solution.py:188
  113.2 4.4 %collective-permute-start = (bf16[128,16,128]{2,1,0:T(8,128)(2,1)S(1)}, bf16[128,16,128]{2,1,0:T(8,128)(2,1)S(1)}, u32[]{:S(2)}, u32[]{:S(2)}) collective-permute-start(bf16[128,16,128]{2,1,0:T(8,128)(2,1)S(1)} %all_to_all.10), channel_id=1, source_target_pairs={{0,1},{1,0},{2,3},{3,2},{4,5},{5,4},{6,7},{7,6},{8,9},{9,8},{10,11... | collective-permute-start | bytes 1572872 | tf_op jit(solution)/shard_map/ppermute | solution.py:192
  118.2 0.0 copy-start.6
  118.2 0.0 copy-start.7
  118.3 0.0 copy-done.3
  118.3 0.6 copy-done.6
  118.9 0.0 copy-done.7
  118.9 0.6 own.1
  119.5 0.0 collective-permute-done
  119.5 0.4 peer.1
  120.0 0.0 copy-start
  120.0 50.4 %all_to_all.11 = bf16[128,8,128]{2,1,0:T(8,128)(2,1)S(1)} all-to-all(bf16[128,8,128]{2,1,0:T(8,128)(2,1)S(1)} %bitcast.10), channel_id=1, replica_groups={{0,3,4,7,8,11,12,15,16,19,20,23,24,27,28,31,32,35,36,39,40,43,44,47,48,..., dimensions={0} | all-to-all | bytes 524288 | tf_op jit(solution)/shard_map/all_to_all | solution.py:188
  170.3 0.0 copy-done
  170.4 1.3 post.1
Async XLA Ops:
  0.0 0.9 copy-start.1
  1.0 0.9 copy-start.2
  1.4 0.7 copy-start.4
  1.4 0.7 copy-start.5
  2.9 115.3 %copy-start.3 = (bf16[128,128]{1,0:T(8,128)(2,1)S(1)}, bf16[128,128]{1,0:T(8,128)(2,1)}, u32[]{:S(2)}) copy-start(bf16[128,128]{1,0:T(8,128)(2,1)} %w_gate.1) | copy-start | bytes 98308
  113.2 6.3 %collective-permute-start = (bf16[128,16,128]{2,1,0:T(8,128)(2,1)S(1)}, bf16[128,16,128]{2,1,0:T(8,128)(2,1)S(1)}, u32[]{:S(2)}, u32[]{:S(2)}) collective-permute-start(bf16[128,16,128]{2,1,0:T(8,128)(2,1)S(1)} %all_to_all.10), channel_id=1, source_target_pairs={{0,1},{1,0},{2,3},{3,2},{4,5},{5,4},{6,7},{7,6},{8,9},{9,8},{10,11... | collective-permute-start | bytes 1572872 | tf_op jit(solution)/shard_map/ppermute | solution.py:192
  118.2 0.7 copy-start.6
  118.2 0.7 copy-start.7
  120.0 50.4 %copy-start = (bf16[128,128]{1,0:T(8,128)(2,1)S(1)}, bf16[128,128]{1,0:T(8,128)(2,1)}, u32[]{:S(2)}) copy-start(bf16[128,128]{1,0:T(8,128)(2,1)} %w_ref.3) | copy-start | bytes 98308

commit v7 on v5

--- a/solution.py
+++ b/solution.py
@@ -18,6 +18,10 @@
 
 def swap_halves(value):
     return pltpu.roll(value, value.shape[-1] // 2, value.ndim - 1)
+
+
+def evens_first(rows, group):
+    return [start + odd for start in range(0, rows, group) for odd in (0, 1)]
 
 
 def center_kernel(x_ref, out_ref, rows_s):
@@ -27,7 +31,8 @@
     spread = jnp.mean(x * x, -1, keepdims=True)
     rows_s[...] = x * lax.rsqrt(spread + EPS)
     for k in range(cols):
-        out_ref[k] = rows_s[pl.ds(k, rows, stride=cols), :]
+        for first, row in enumerate(evens_first(rows, cols)):
+            out_ref[k, pl.ds(8 * first, 8)] = rows_s[pl.ds(row * cols + k, 8, stride=2 * cols), :]
 
 
 def pre_kernel(x_ref, gain, bias, w_ref, normed_ref, out_ref, out_s):
@@ -53,7 +58,9 @@
     parts = [ref[:, x].reshape(steps * depth, lanes)[:, first : first + half] for x in range(blocks)]
     value = jnp.concatenate(parts, 1)
     lane = lax.broadcasted_iota(jnp.int32, (1, blocks * half), 1)
-    live = lane // half * (lax.axis_size("gz") * half) + core * half + lane % half < length
+    slot = lane % depth
+    row = lane % half - slot + slot % (depth // 2) * 2 + slot // (depth // 2)
+    live = lane // half * (lax.axis_size("gz") * half) + core * half + row < length
     if mask_k:
         live = live & (lax.broadcasted_iota(jnp.int32, (steps * depth, 1), 0) < length)
     return value * jnp.where(live, 1.0, 0.0).astype(jnp.bfloat16)
@@ -99,34 +106,31 @@
 
 
 def post_kernel(t_ref, gate, gain_t, bias_t, w_ref, out_hbm, t_s, out_s, out_v, sems):
-    rows, cols, width = out_v.shape
+    parts, rows, part, width = out_v.shape
     hidden = w_ref.shape[0]
+    cols = parts * part
     depth = cols // 2
     t_s[...] = t_ref[...].astype(jnp.float32).reshape(t_s.shape)
     w = w_ref[...]
+    copies = []
     for r in range(depth):
         t = t_s[pl.ds(r, hidden, stride=depth), :]
         t = t - jnp.mean(t, 0, keepdims=True)
         spread = jnp.mean(t * t, 0, keepdims=True)
         t = (t * lax.rsqrt(spread + EPS) * gain_t[...] + bias_t[...]).astype(jnp.bfloat16)
         o = lax.dot_general(t, w, TN, preferred_element_type=jnp.float32)
-        for half, col in enumerate((r, depth + r)):
-            here = slice(half * rows, (half + 1) * rows)
-            out_s[pl.ds(col, rows, stride=cols), :] = gate[pl.ds(col * rows, rows)] * o[here]
-    parts = sems.shape[0]
-    step = rows // parts
-    copies = []
-    for p in range(parts):
-        here = pl.ds(p * step * cols, step * cols)
-        out_v[pl.ds(p * step, step)] = (
-            out_s[here].astype(jnp.bfloat16).reshape(step, cols, width)
-        )
-        copies.append(
-            pltpu.make_async_copy(
-                out_v.at[pl.ds(p * step, step)], out_hbm.at[pl.ds(p * step, step)], sems.at[p]
+        for half in (0, 1):
+            col = 2 * r + half
+            value = gate[pl.ds(col * rows, rows)] * o[half * rows : (half + 1) * rows]
+            p, here = divmod(col, part)
+            for first, row in enumerate(evens_first(rows, cols)):
+                out_s[p, pl.ds(row * part + here, 8, stride=2 * part), :] = value[8 * first : 8 * first + 8]
+        if (2 * r + 2) % part == 0:
+            out_v[p] = out_s[p].astype(jnp.bfloat16).reshape(rows, part, width)
+            copies.append(
+                pltpu.make_async_copy(out_v.at[p], out_hbm.at[:, pl.ds(p * part, part)], sems.at[p])
             )
-        )
-        copies[-1].start()
+            copies[-1].start()
     for copy in copies:
         copy.wait()
 
@@ -142,7 +146,7 @@
     rows, cols, width = pair.shape
     hidden = w_out.shape[0]
     steps, blocks, cores = (lax.axis_size(a) for a in ("gy", "gx", "gz"))
-    parts = 4
+    parts = 2
     flat, square = (rows * cols, width), (hidden, 2 * rows)
     centered = pl.pallas_call(
         center_kernel,
@@ -206,8 +210,8 @@
         out_specs=HBM,
         scratch_shapes=[
             pltpu.VMEM((hidden * cols // 2, 2 * rows), jnp.float32),
-            pltpu.VMEM(flat, jnp.float32),
-            pltpu.VMEM((rows, cols, width), jnp.bfloat16),
+            pltpu.VMEM((parts, rows * cols // parts, width), jnp.float32),
+            pltpu.VMEM((parts, rows, cols // parts, width), jnp.bfloat16),
             pltpu.SemaphoreType.DMA((parts,)),
         ],
         compiler_params=PARAMS,

time: 172 us -> 172 us (level)
  no operation moved by 1% of the time
where the time goes in v7:
time: 172 us
  blocking collectives  163 us (95%)
  Pallas kernels  3.67 us (2%)
  local copies, waits for them, and re-layouts  2.28 us (1%)
  starting transfers between devices  1.94 us (1%)
    all_to_all x1, blocking collectives, body(): own = lax.all_to_all(operands, ('gy', 'gx'), 0, 0, tiled=True)  113 us
    all_to_all x1, blocking collectives, body(): back = lax.all_to_all(tiles, ('gy', 'gx'), 0, 0, tiled=True)  50.7 us
  transfers between devices with their start and end apart: 1, of which 0 were waited for; matrix products, arithmetic and copies ran while one was open for 0% of the time, Pallas kernels for 0%

profile of v7, /device:TPU:38, one launch (start us, length us, event | category | flops | bytes accessed | tf_op | source)
XLA Modules:
  0.0 171.8 jit_solution(16069915192946698372)
XLA Ops:
  0.0 0.0 copy-start.1
  0.0 0.9 copy-done.1
  1.0 0.0 copy-start.2
  1.0 0.6 center.1.x_ref
  1.6 0.0 copy-start.4
  1.6 0.0 copy-start.5
  1.6 0.2 copy-done.2
  1.9 0.4 copy-done.4
  2.3 0.0 copy-done.5
  2.3 0.8 pre.1
  3.1 0.0 copy-start.3
  3.1 112.5 %all_to_all.10 = bf16[128,16,128]{2,1,0:T(8,128)(2,1)S(1)} all-to-all(bf16[128,16,128]{2,1,0:T(8,128)(2,1)S(1)} %get-tuple-element.14), channel_id=1, replica_groups=mesh['grp'=2,'gy'=32,'gx'=4,'gz'=2] {'gy','gx'}, dimensions={0} | all-to-all | bytes 1048576 | tf_op jit(solution)/shard_map/all_to_all | solution.py:174
  115.7 1.9 %collective-permute-start = (bf16[128,16,128]{2,1,0:T(8,128)(2,1)S(1)}, bf16[128,16,128]{2,1,0:T(8,128)(2,1)S(1)}, u32[]{:S(2)}, u32[]{:S(2)}) collective-permute-start(bf16[128,16,128]{2,1,0:T(8,128)(2,1)S(1)} %all_to_all.10), channel_id=1, source_target_pairs={{0,1},{1,0},{2,3},{3,2},{4,5},{5,4},{6,7},{7,6},{8,9},{9,8},{10,11... | collective-permute-start | bytes 1572872 | tf_op jit(solution)/shard_map/ppermute | solution.py:176
  118.2 0.0 copy-start.6
  118.3 0.0 copy-start.7
  118.3 0.0 copy-done.3
  118.3 0.6 copy-done.6
  118.9 0.0 copy-done.7
  118.9 0.6 own.1
  119.5 0.0 collective-permute-done
  119.5 0.4 peer.1
  120.0 0.0 copy-start
  120.0 50.7 %all_to_all.11 = bf16[128,8,128]{2,1,0:T(8,128)(2,1)S(1)} all-to-all(bf16[128,8,128]{2,1,0:T(8,128)(2,1)S(1)} %bitcast.10), channel_id=1, replica_groups=mesh['grp'=2,'gy'=32,'gx'=4,'gz'=2] {'gy','gx'}, dimensions={0} | all-to-all | bytes 524288 | tf_op jit(solution)/shard_map/all_to_all | solution.py:205
  170.6 0.0 copy-done
  170.6 1.2 post.1
Async XLA Ops:
  0.0 0.9 copy-start.1
  1.0 0.9 copy-start.2
  1.6 0.7 copy-start.4
  1.6 0.7 copy-start.5
  3.1 115.2 %copy-start.3 = (bf16[128,128]{1,0:T(8,128)(2,1)S(1)}, bf16[128,128]{1,0:T(8,128)(2,1)}, u32[]{:S(2)}) copy-start(bf16[128,128]{1,0:T(8,128)(2,1)} %w_gate.1) | copy-start | bytes 98308
  115.7 3.9 %collective-permute-start = (bf16[128,16,128]{2,1,0:T(8,128)(2,1)S(1)}, bf16[128,16,128]{2,1,0:T(8,128)(2,1)S(1)}, u32[]{:S(2)}, u32[]{:S(2)}) collective-permute-start(bf16[128,16,128]{2,1,0:T(8,128)(2,1)S(1)} %all_to_all.10), channel_id=1, source_target_pairs={{0,1},{1,0},{2,3},{3,2},{4,5},{5,4},{6,7},{7,6},{8,9},{9,8},{10,11... | collective-permute-start | bytes 1572872 | tf_op jit(solution)/shard_map/ppermute | solution.py:176
  118.2 0.7 copy-start.6
  118.3 0.7 copy-start.7
  120.0 50.7 %copy-start = (bf16[128,128]{1,0:T(8,128)(2,1)S(1)}, bf16[128,128]{1,0:T(8,128)(2,1)}, u32[]{:S(2)}) copy-start(bf16[128,128]{1,0:T(8,128)(2,1)} %w_ref.3) | copy-start | bytes 98308

commit v8 on v7

--- a/solution.py
+++ b/solution.py
@@ -24,24 +24,21 @@
     return [start + odd for start in range(0, rows, group) for odd in (0, 1)]
 
 
-def center_kernel(x_ref, out_ref, rows_s):
-    cols, rows, width = out_ref.shape
-    x = x_ref[...].reshape(rows * cols, width).astype(jnp.float32)
+def center_kernel(x_ref, out_ref):
+    x = x_ref[...].reshape(out_ref.shape).astype(jnp.float32)
     x = x - jnp.mean(x, -1, keepdims=True)
     spread = jnp.mean(x * x, -1, keepdims=True)
-    rows_s[...] = x * lax.rsqrt(spread + EPS)
-    for k in range(cols):
-        for first, row in enumerate(evens_first(rows, cols)):
-            out_ref[k, pl.ds(8 * first, 8)] = rows_s[pl.ds(row * cols + k, 8, stride=2 * cols), :]
+    out_ref[...] = x * lax.rsqrt(spread + EPS)
 
 
 def pre_kernel(x_ref, gain, bias, w_ref, normed_ref, out_ref, out_s):
-    cols, rows, width = x_ref.shape
-    hidden = out_ref.shape[0]
+    hidden, cols, rows = out_ref.shape
+    rows = rows // 2
     w_t = w_ref[...].astype(jnp.float32).T.astype(jnp.bfloat16)
     low = low_half((1, 2 * rows))
     for k in range(0, cols, 2):
-        block = x_ref[pl.ds(k, 2)].reshape(2 * rows, width)
+        starts = [row * cols + col for col in (k, k + 1) for row in evens_first(rows, cols)]
+        block = jnp.concatenate([x_ref[pl.ds(start, 8, stride=2 * cols), :] for start in starts], 0)
         block = (block * gain[...] + bias[...]).astype(jnp.bfloat16)
         normed_ref[pl.ds(k * rows, 2 * rows)] = block
         proj = lax.dot_general(w_t, block, NT, preferred_element_type=jnp.float32)
@@ -150,10 +147,9 @@
     flat, square = (rows * cols, width), (hidden, 2 * rows)
     centered = pl.pallas_call(
         center_kernel,
-        out_shape=jax.ShapeDtypeStruct((cols, rows, width), jnp.float32),
+        out_shape=jax.ShapeDtypeStruct(flat, jnp.float32),
         in_specs=[VMEM],
         out_specs=VMEM,
-        scratch_shapes=[pltpu.VMEM(flat, jnp.float32)],
         compiler_params=PARAMS,
         cost_estimate=COST,
         name="center",

time: 172 us -> 172 us (level)
  no operation moved by 1% of the time
where the time goes in v8:
time: 172 us
  blocking collectives  163 us (95%)
  Pallas kernels  3.4 us (2%)
  local copies, waits for them, and re-layouts  2.28 us (1%)
  starting transfers between devices  1.94 us (1%)
    all_to_all x1, blocking collectives, body(): own = lax.all_to_all(operands, ('gy', 'gx'), 0, 0, tiled=True)  113 us
    all_to_all x1, blocking collectives, body(): back = lax.all_to_all(tiles, ('gy', 'gx'), 0, 0, tiled=True)  50.7 us
  transfers between devices with their start and end apart: 1, of which 0 were waited for; matrix products, arithmetic and copies ran while one was open for 0% of the time, Pallas kernels for 0%

profile of v8, /device:TPU:38, one launch (start us, length us, event | category | flops | bytes accessed | tf_op | source)
XLA Modules:
  0.0 171.6 jit_solution(18007573672141012956)
XLA Ops:
  0.0 0.0 copy-start.1
  0.0 0.9 copy-done.1
  1.0 0.0 copy-start.2
  1.0 0.3 center.1.x_ref
  1.3 0.0 copy-start.4
  1.3 0.0 copy-start.5
  1.3 0.5 copy-done.2
  1.9 0.1 copy-done.4
  2.0 0.0 copy-done.5
  2.0 0.8 pre.1
  2.8 0.0 copy-start.3
  2.9 112.5 %all_to_all.10 = bf16[128,16,128]{2,1,0:T(8,128)(2,1)S(1)} all-to-all(bf16[128,16,128]{2,1,0:T(8,128)(2,1)S(1)} %get-tuple-element.14), channel_id=1, replica_groups=mesh['grp'=2,'gy'=32,'gx'=4,'gz'=2] {'gy','gx'}, dimensions={0} | all-to-all | bytes 1048576 | tf_op jit(solution)/shard_map/all_to_all | solution.py:170
  115.4 1.9 %collective-permute-start = (bf16[128,16,128]{2,1,0:T(8,128)(2,1)S(1)}, bf16[128,16,128]{2,1,0:T(8,128)(2,1)S(1)}, u32[]{:S(2)}, u32[]{:S(2)}) collective-permute-start(bf16[128,16,128]{2,1,0:T(8,128)(2,1)S(1)} %all_to_all.10), channel_id=1, source_target_pairs={{0,1},{1,0},{2,3},{3,2},{4,5},{5,4},{6,7},{7,6},{8,9},{9,8},{10,11... | collective-permute-start | bytes 1572872 | tf_op jit(solution)/shard_map/ppermute | solution.py:172
  118.0 0.0 copy-start.6
  118.0 0.0 copy-start.7
  118.0 0.0 copy-done.3
  118.0 0.6 copy-done.6
  118.6 0.0 copy-done.7
  118.7 0.6 own.1
  119.3 0.0 collective-permute-done
  119.3 0.4 peer.1
  119.7 0.0 copy-start
  119.7 50.7 %all_to_all.11 = bf16[128,8,128]{2,1,0:T(8,128)(2,1)S(1)} all-to-all(bf16[128,8,128]{2,1,0:T(8,128)(2,1)S(1)} %bitcast.10), channel_id=1, replica_groups=mesh['grp'=2,'gy'=32,'gx'=4,'gz'=2] {'gy','gx'}, dimensions={0} | all-to-all | bytes 524288 | tf_op jit(solution)/shard_map/all_to_all | solution.py:201
  170.4 0.0 copy-done
  170.4 1.2 post.1
Async XLA Ops:
  0.0 0.9 copy-start.1
  1.0 0.9 copy-start.2
  1.3 0.7 copy-start.4
  1.3 0.7 copy-start.5
  2.8 115.2 %copy-start.3 = (bf16[128,128]{1,0:T(8,128)(2,1)S(1)}, bf16[128,128]{1,0:T(8,128)(2,1)}, u32[]{:S(2)}) copy-start(bf16[128,128]{1,0:T(8,128)(2,1)} %w_gate.1) | copy-start | bytes 98308
  115.4 3.9 %collective-permute-start = (bf16[128,16,128]{2,1,0:T(8,128)(2,1)S(1)}, bf16[128,16,128]{2,1,0:T(8,128)(2,1)S(1)}, u32[]{:S(2)}, u32[]{:S(2)}) collective-permute-start(bf16[128,16,128]{2,1,0:T(8,128)(2,1)S(1)} %all_to_all.10), channel_id=1, source_target_pairs={{0,1},{1,0},{2,3},{3,2},{4,5},{5,4},{6,7},{7,6},{8,9},{9,8},{10,11... | collective-permute-start | bytes 1572872 | tf_op jit(solution)/shard_map/ppermute | solution.py:172
  118.0 0.7 copy-start.6
  118.0 0.7 copy-start.7
  119.7 50.7 %copy-start = (bf16[128,128]{1,0:T(8,128)(2,1)S(1)}, bf16[128,128]{1,0:T(8,128)(2,1)}, u32[]{:S(2)}) copy-start(bf16[128,128]{1,0:T(8,128)(2,1)} %w_ref.3) | copy-start | bytes 98308

commit v9 on v8

--- a/solution.py
+++ b/solution.py
@@ -18,6 +18,10 @@
 
 def swap_halves(value):
     return pltpu.roll(value, value.shape[-1] // 2, value.ndim - 1)
+
+
+def sigmoid(value):
+    return 0.5 * jnp.tanh(0.5 * value) + 0.5
 
 
 def evens_first(rows, group):
@@ -42,8 +46,8 @@
         block = (block * gain[...] + bias[...]).astype(jnp.bfloat16)
         normed_ref[pl.ds(k * rows, 2 * rows)] = block
         proj = lax.dot_general(w_t, block, NT, preferred_element_type=jnp.float32)
-        left = jax.nn.sigmoid(proj[:hidden]) * proj[hidden : 2 * hidden]
-        right = jax.nn.sigmoid(proj[2 * hidden : 3 * hidden]) * proj[3 * hidden :]
+        left = sigmoid(proj[:hidden]) * proj[hidden : 2 * hidden]
+        right = sigmoid(proj[2 * hidden : 3 * hidden]) * proj[3 * hidden :]
         out_s[pl.ds(k, hidden, stride=cols), :] = jnp.where(low, left, swap_halves(right))
         out_s[pl.ds(k + 1, hidden, stride=cols), :] = jnp.where(low, swap_halves(left), right)
     out_ref[...] = out_s[...].astype(jnp.bfloat16).reshape(out_ref.shape)
@@ -88,7 +92,7 @@
     tiles = product(left, operand(own_ref, half, length[0], core, False), own_ref.shape[2])
     for pair, tile in enumerate(tiles):
         out_ref[:, :, pair] = tile
-    gate_ref[...] = jax.nn.sigmoid(jnp.dot(normed[...], w_gate[...], preferred_element_type=jnp.float32))
+    gate_ref[...] = sigmoid(jnp.dot(normed[...], w_gate[...], preferred_element_type=jnp.float32))
     gain_t[...] = jnp.broadcast_to(gain[...], gain_t.shape[::-1]).T
     bias_t[...] = jnp.broadcast_to(bias[...], bias_t.shape[::-1]).T
 

time: 172 us -> 172 us (level)
  no operation moved by 1% of the time
where the time goes in v9:
time: 172 us
  blocking collectives  163 us (95%)
  Pallas kernels  3.48 us (2%)
  local copies, waits for them, and re-layouts  2.28 us (1%)
  starting transfers between devices  1.94 us (1%)
    all_to_all x1, blocking collectives, body(): own = lax.all_to_all(operands, ('gy', 'gx'), 0, 0, tiled=True)  113 us
    all_to_all x1, blocking collectives, body(): back = lax.all_to_all(tiles, ('gy', 'gx'), 0, 0, tiled=True)  50.7 us
  transfers between devices with their start and end apart: 1, of which 0 were waited for; matrix products, arithmetic and copies ran while one was open for 0% of the time, Pallas kernels for 0%

profile of v9, /device:TPU:38, one launch (start us, length us, event | category | flops | bytes accessed | tf_op | source)
XLA Modules:
  0.0 171.6 jit_solution(7007183018483320041)
XLA Ops:
  0.0 0.0 copy-start.1
  0.0 0.9 copy-done.1
  1.0 0.0 copy-start.2
  1.0 0.3 center.1.x_ref
  1.3 0.0 copy-start.4
  1.3 0.0 copy-start.5
  1.3 0.5 copy-done.2
  1.9 0.1 copy-done.4
  2.0 0.0 copy-done.5
  2.0 0.9 pre.1
  2.9 0.0 copy-start.3
  2.9 112.5 %all_to_all.10 = bf16[128,16,128]{2,1,0:T(8,128)(2,1)S(1)} all-to-all(bf16[128,16,128]{2,1,0:T(8,128)(2,1)S(1)} %get-tuple-element.14), channel_id=1, replica_groups=mesh['grp'=2,'gy'=32,'gx'=4,'gz'=2] {'gy','gx'}, dimensions={0} | all-to-all | bytes 1048576 | tf_op jit(solution)/shard_map/all_to_all | solution.py:174
  115.5 1.9 %collective-permute-start = (bf16[128,16,128]{2,1,0:T(8,128)(2,1)S(1)}, bf16[128,16,128]{2,1,0:T(8,128)(2,1)S(1)}, u32[]{:S(2)}, u32[]{:S(2)}) collective-permute-start(bf16[128,16,128]{2,1,0:T(8,128)(2,1)S(1)} %all_to_all.10), channel_id=1, source_target_pairs={{0,1},{1,0},{2,3},{3,2},{4,5},{5,4},{6,7},{7,6},{8,9},{9,8},{10,11... | collective-permute-start | bytes 1572872 | tf_op jit(solution)/shard_map/ppermute | solution.py:176
  118.1 0.0 copy-start.6
  118.1 0.0 copy-start.7
  118.1 0.0 copy-done.3
  118.1 0.6 copy-done.6
  118.7 0.0 copy-done.7
  118.7 0.6 own.1
  119.3 0.0 collective-permute-done
  119.3 0.4 peer.1
  119.8 0.0 copy-start
  119.8 50.7 %all_to_all.11 = bf16[128,8,128]{2,1,0:T(8,128)(2,1)S(1)} all-to-all(bf16[128,8,128]{2,1,0:T(8,128)(2,1)S(1)} %bitcast.10), channel_id=1, replica_groups=mesh['grp'=2,'gy'=32,'gx'=4,'gz'=2] {'gy','gx'}, dimensions={0} | all-to-all | bytes 524288 | tf_op jit(solution)/shard_map/all_to_all | solution.py:205
  170.4 0.0 copy-done
  170.4 1.2 post.1
Async XLA Ops:
  0.0 0.9 copy-start.1
  1.0 0.9 copy-start.2
  1.3 0.7 copy-start.4
  1.3 0.7 copy-start.5
  2.9 115.2 %copy-start.3 = (bf16[128,128]{1,0:T(8,128)(2,1)S(1)}, bf16[128,128]{1,0:T(8,128)(2,1)}, u32[]{:S(2)}) copy-start(bf16[128,128]{1,0:T(8,128)(2,1)} %w_gate.1) | copy-start | bytes 98308
  115.5 3.9 %collective-permute-start = (bf16[128,16,128]{2,1,0:T(8,128)(2,1)S(1)}, bf16[128,16,128]{2,1,0:T(8,128)(2,1)S(1)}, u32[]{:S(2)}, u32[]{:S(2)}) collective-permute-start(bf16[128,16,128]{2,1,0:T(8,128)(2,1)S(1)} %all_to_all.10), channel_id=1, source_target_pairs={{0,1},{1,0},{2,3},{3,2},{4,5},{5,4},{6,7},{7,6},{8,9},{9,8},{10,11... | collective-permute-start | bytes 1572872 | tf_op jit(solution)/shard_map/ppermute | solution.py:176
  118.1 0.7 copy-start.6
  118.1 0.7 copy-start.7
  119.8 50.7 %copy-start = (bf16[128,128]{1,0:T(8,128)(2,1)S(1)}, bf16[128,128]{1,0:T(8,128)(2,1)}, u32[]{:S(2)}) copy-start(bf16[128,128]{1,0:T(8,128)(2,1)} %w_ref.3) | copy-start | bytes 98308
